TPU v7x, 256 devices: a whole 4x4x8 slice. The times are simulated.
256 devices in a mesh: rep: 16 (over x, z_hi, core), stripe: 16 (over y, z_lo).
Axes of the slice: x: 4, y: 4, z: 8 (z_hi: 2, z_lo: 4; z = z_hi * 4 + z_lo), core: 2. Of those that a mesh axis runs over, the one named last changes fastest.
Arguments:
- activations: bfloat16 [4096, 4096], P('rep'), may hold values from -6 to 6
- out_grads: bfloat16 [4096, 8192], P('rep', 'stripe'), may hold values from -4 to 4
- statistics: float32 [16, 16, 512, 512], P('rep', 'stripe'), may hold values from -48 to 4608, as said below
- owner_blocks: int32 [16, 8], P('stripe'), may hold values from 0 to 7, each once within a row
Outputs:
- preconditioned: float32 [4096, 8192], P(None, 'stripe')
- new_stats: float32 [16, 16, 512, 512], P('rep', 'stripe')
Inputs may be any that keep to these rules, and one draw needn't show every extreme that they name: statistics[p, s] is symmetric positive definite for every p and s. `owner_blocks`: each row lists every row block 0 to 7 exactly once.
All inputs are finite; a program needn't handle non-finite values.
Results may differ from a plain program's by a relative error of at most 0.0003.
Values sent between devices are 32-bit elements; how exact they have to be, the bound alone decides.
A program may use at most 128 MiB of HBM per device.

v0:
```python
import jax
import jax.numpy as jnp
from jax import lax
from jax.sharding import Mesh
from jax.sharding import PartitionSpec as P

BLOCK = 512
ITERS = 2
REP = ("rep_0", "rep_1", "rep_2")
REP_STRIPE = ("rep_0", "rep_1", "rep_2", "stripe_0", "stripe_1")
STRIPE = ("stripe_0", "stripe_1")


decay_rate = 0.95
damping = 0.25
epsilon = 1e-06
highest = lax.Precision.HIGHEST


def partner(shard, axis, stride):
    return lax.ppermute(shard, axis, [(i, i ^ 1 << stride) for i in range(lax.axis_size(axis))])


def by_axis(shard, axes):
    for axis in axes:
        shard = lax.psum(shard, axis)
    return shard


def inverse_root(damped):
    identity = jnp.eye(damped.shape[-1], dtype=damped.dtype)
    frob_norm = jnp.sqrt(jnp.sum(damped * damped, axis=(-2, -1), keepdims=True) + epsilon)
    scaled = damped / frob_norm
    root_now = identity * frob_norm ** (-0.25)
    for sweep in range(ITERS):
        factor = (5.0 * identity - scaled) * 0.25
        root_now = jnp.matmul(root_now, factor, precision=highest)
        if sweep + 1 < ITERS:
            square = jnp.matmul(factor, factor, precision=highest)
            fourth = jnp.matmul(square, square, precision=highest)
            scaled = jnp.matmul(fourth, scaled, precision=highest)
    return root_now


def slot_terms(activations, out_grads, blocks_of, pair_count, piece_rows, row_count):
    tokens_here, in_width = activations.shape
    per_block = BLOCK // piece_rows
    shaped = activations.reshape(tokens_here, in_width // piece_rows, piece_rows)
    slot_count = row_count // piece_rows
    slot_ids = jnp.arange(slot_count, dtype=jnp.int32)
    block_ids = jnp.take(blocks_of, slot_ids % pair_count)
    half_ids = slot_ids // pair_count % per_block
    chosen = jnp.take(shaped, block_ids * per_block + half_ids, axis=1)
    products = jnp.einsum("tkp,tc->kpc", chosen, out_grads, preferred_element_type=jnp.float32)
    return products.reshape(slot_count * piece_rows, out_grads.shape[1])


def per_device(activations, out_grads, statistics, owner_blocks):
    rep_count = lax.axis_size(REP)
    pair_count = rep_count // 2
    pair_bit = rep_count.bit_length() - 2
    half_rows = BLOCK // 2
    my_index = lax.axis_index(REP)
    is_left = my_index < pair_count
    blocks_of = owner_blocks[0]
    own_half = lax.psum_scatter(
        slot_terms(
            activations, out_grads, blocks_of, pair_count, half_rows, half_rows * lax.axis_size(REP)
        ),
        REP,
        scatter_dimension=0,
        tiled=True,
    )
    partner_half = partner(own_half, REP, pair_bit)
    gradient = jnp.where(
        is_left,
        jnp.concatenate([own_half, partner_half], axis=0),
        jnp.concatenate([partner_half, own_half], axis=0),
    )
    facing = jnp.where(is_left, gradient, gradient.T)
    new_stat = decay_rate * statistics[0, 0] + jnp.dot(facing, facing.T, precision=highest)
    trace_sum = by_axis(jnp.trace(new_stat), REP_STRIPE)
    mean_diag = trace_sum / (rep_count * lax.axis_size(STRIPE) * BLOCK)
    identity = jnp.eye(BLOCK, dtype=jnp.float32)
    root_now = inverse_root(new_stat + damping * mean_diag * identity)
    partner_root = partner(root_now, REP, pair_bit)
    left_root = jnp.where(is_left, root_now, partner_root)
    right_root = jnp.where(is_left, partner_root, root_now)
    row_start = jnp.where(is_left, 0, half_rows).astype(jnp.int32)
    my_rows = lax.dynamic_slice_in_dim(left_root, row_start, half_rows, 0)
    grad_rows = lax.dynamic_slice_in_dim(gradient, row_start, half_rows, 0)
    precond_half = jnp.dot(
        jnp.dot(my_rows, gradient, precision=highest), right_root, precision=highest
    )
    grad_sq, prec_sq = (
        by_axis(jnp.sum(grad_rows * grad_rows), REP_STRIPE),
        by_axis(jnp.sum(precond_half * precond_half), REP_STRIPE),
    )
    scaled = precond_half * jnp.sqrt(grad_sq / (prec_sq + epsilon))
    gathered = lax.all_gather(scaled[None], REP, axis=0, tiled=True)
    pair_ids = jnp.arange(pair_count, dtype=jnp.int32)
    inverse = jnp.sum(
        pair_ids[:, None] * (blocks_of[:, None] == pair_ids[None, :]).astype(jnp.int32), axis=0
    )
    row_order = jnp.stack([inverse, inverse + pair_count], axis=1).reshape(-1)
    preconditioned = jnp.take(gathered, row_order, axis=0).reshape(
        pair_count * BLOCK, gathered.shape[2]
    )
    return (preconditioned, new_stat[None, None])


def solution(mesh):
    split = Mesh(
        mesh.devices.reshape(4, 2, 2, 4, 4), ("rep_0", "rep_1", "rep_2", "stripe_0", "stripe_1")
    )
    return jax.shard_map(
        per_device,
        mesh=split,
        in_specs=(P(REP, None), P(REP, STRIPE), P(REP, STRIPE, None, None), P(STRIPE, None)),
        out_specs=(P(None, STRIPE), P(REP, STRIPE, None, None)),
        check_vma=False,
    )
```

profile of v0, /device:TPU:1, one launch (start us, length us, event | category | flops | bytes accessed | tf_op | source)
XLA Modules:
  0.0 449.1 jit_solution(16025409931431591571)
XLA Ops:
  8.2 1.3 gather_fusion
  9.6 4.1 copy.26
  13.7 2.8 copy.27
  16.5 2.0 gather_fusion.1
  18.5 6.7 %fusion = f32[16,256,512]{2,1,0:T(8,128)} fusion(bf16[16,256,256]{2,1,0:T(8,128)(2,1)} %gather_fusion.1, pred[16]{0:T(512)(128)(4,1)S(1)} %get-tuple-element.16, bf16[256,512]{1,0:T(8,128)(2,1)S(1)} %copy-done), kind=kOutput, calls=%fused_computation.4 | convolution fusion | flops 1074790400 | bytes 10747920 | tf_op jit(solution)/shard_map/tkp,tc->kpc/dot_general | solution.py:54
  25.2 8.9 %copy.29 = f32[4096,512]{0,1:T(8,128)} copy(f32[4096,512]{1,0:T(8,128)} %bitcast.40) | data formatting | bytes 16777216 | tf_op jit(solution)/shard_map/reshape | solution.py:55
  34.2 142.1 %reduce-scatter.2.cloned.1.call-done = f32[256,512]{0,1:T(8,128)} async-done(((f32[4096,512]{0,1:T(8,128)}), f32[256,512]{0,1:T(8,128)}) %reduce-scatter.2.cloned.1.call-update) | async-done | bytes 524304 | tf_op jit(solution)/shard_map/reduce_scatter | solution.py:66
  176.3 1.2 collective-permute-start
  177.5 11.7 %collective-permute-done = f32[256,512]{0,1:T(8,128)S(1)} collective-permute-done((f32[256,512]{0,1:T(8,128)}, f32[256,512]{0,1:T(8,128)S(1)}, u32[]{:S(2)}, u32[]{:S(2)}) %collective-permute-start) | collective-permute-done | bytes 524320 | tf_op jit(solution)/shard_map/ppermute | solution.py:21
  189.3 1.6 maximum_select_fusion
  191.2 5.6 %select_reduce_fusion = (f32[]{:T(128)}, f32[512,512]{1,0:T(8,128)S(1)}) fusion(f32[512,512]{1,0:T(8,128)S(1)} %copy.31, pred[]{:T(512)S(6)} %lt.75, f32[256,512]{0,1:T(8,128)} %reduce-scatter.2.cloned.1.call-done, f32[256,512]{0,1:T(8,128)} %copy-done.3, f32[1,1,512,512]{3,2,1,0:T(8,128)} %param.6), kind=kOutput, calls=%fused_computation.22 | convolution fusion | flops 1612972032 | bytes 4194309 | tf_op jit(solution)/shard_map/dot_general | solution.py:81
  196.8 6.6 %psum.105 = f32[]{:T(128)} all-reduce(f32[]{:T(128)} %get-tuple-element.12), channel_id=1, replica_groups=mesh['rep_0'=4,'rep_1'=2,'rep_2'=2,'stripe_0'=4,'stripe_1'=4] {'rep_0'}, use_global_device_ids=true, to_apply=%region_3.4 | all-reduce | flops 1 | bytes 8 | tf_op jit(solution)/shard_map/psum | solution.py:26
  203.4 8.3 %psum.106 = f32[]{:T(128)} all-reduce(f32[]{:T(128)} %psum.105), channel_id=1, replica_groups=mesh['rep_0'=4,'rep_1'=2,'rep_2'=2,'stripe_0'=4,'stripe_1'=4] {'rep_1'}, use_global_device_ids=true, to_apply=%region_4.5 | all-reduce | flops 1 | bytes 8 | tf_op jit(solution)/shard_map/psum | solution.py:26
  211.6 9.8 %psum.107 = f32[]{:T(128)} all-reduce(f32[]{:T(128)} %psum.106), channel_id=1, replica_groups=mesh['rep_0'=4,'rep_1'=2,'rep_2'=2,'stripe_0'=4,'stripe_1'=4] {'rep_2'}, use_global_device_ids=true, to_apply=%region_5.6 | all-reduce | flops 1 | bytes 8 | tf_op jit(solution)/shard_map/psum | solution.py:26
  221.4 7.5 %psum.108 = f32[]{:T(128)} all-reduce(f32[]{:T(128)} %psum.107), channel_id=1, replica_groups=mesh['rep_0'=4,'rep_1'=2,'rep_2'=2,'stripe_0'=4,'stripe_1'=4] {'stripe_0'}, use_global_device_ids=true, to_apply=%region_6.7 | all-reduce | flops 1 | bytes 8 | tf_op jit(solution)/shard_map/psum | solution.py:26
  228.9 10.8 %psum.109 = f32[]{:T(128)} all-reduce(f32[]{:T(128)} %psum.108), channel_id=1, replica_groups=mesh['rep_0'=4,'rep_1'=2,'rep_2'=2,'stripe_0'=4,'stripe_1'=4] {'stripe_1'}, use_global_device_ids=true, to_apply=%region_7.8 | all-reduce | flops 1 | bytes 8 | tf_op jit(solution)/shard_map/psum | solution.py:26
  242.0 2.0 fusion.12
  244.0 1.8 fusion.46
  245.8 1.9 fusion.4
  247.8 3.1 fusion.9
  250.9 1.8 fusion.47
  254.2 20.9 %collective-permute-done.1 = f32[512,512]{1,0:T(8,128)S(1)} collective-permute-done((f32[512,512]{1,0:T(8,128)S(1)}, f32[512,512]{1,0:T(8,128)S(1)}, u32[]{:S(2)}, u32[]{:S(2)}) %collective-permute-start.1) | collective-permute-done | bytes 1048608 | tf_op jit(solution)/shard_map/ppermute | solution.py:21
  275.0 2.7 fusion.15
  277.8 1.8 multiply_reduce_fusion.1
  279.5 6.6 %all-reduce.2 = (f32[]{:T(128)}, f32[]{:T(128)}) all-reduce(f32[]{:T(128)} %multiply_reduce_fusion.2, f32[]{:T(128)} %get-tuple-element.14), channel_id=1, replica_groups=mesh['rep_0'=4,'rep_1'=2,'rep_2'=2,'stripe_0'=4,'stripe_1'=4] {'rep_0'}, use_global_device_ids=true, to_apply=%region_10.11 | all-reduce | flops 2 | bytes 16 | tf_op jit(solution)/shard_map/psum | solution.py:26
  286.1 8.4 %all-reduce.4 = (f32[]{:T(128)}, f32[]{:T(128)}) all-reduce(f32[]{:T(128)} %get-tuple-element.6, f32[]{:T(128)} %get-tuple-element.7), channel_id=1, replica_groups=mesh['rep_0'=4,'rep_1'=2,'rep_2'=2,'stripe_0'=4,'stripe_1'=4] {'rep_1'}, use_global_device_ids=true, to_apply=%region_11.12 | all-reduce | flops 2 | bytes 16 | tf_op jit(solution)/shard_map/psum | solution.py:26
  294.5 10.6 %all-reduce.3 = (f32[]{:T(128)}, f32[]{:T(128)}) all-reduce(f32[]{:T(128)} %get-tuple-element.10, f32[]{:T(128)} %get-tuple-element.11), channel_id=1, replica_groups=mesh['rep_0'=4,'rep_1'=2,'rep_2'=2,'stripe_0'=4,'stripe_1'=4] {'rep_2'}, use_global_device_ids=true, to_apply=%region_12.13 | all-reduce | flops 2 | bytes 16 | tf_op jit(solution)/shard_map/psum | solution.py:26
  305.1 6.8 %all-reduce.1 = (f32[]{:T(128)}, f32[]{:T(128)}) all-reduce(f32[]{:T(128)} %get-tuple-element.8, f32[]{:T(128)} %get-tuple-element.9), channel_id=1, replica_groups=mesh['rep_0'=4,'rep_1'=2,'rep_2'=2,'stripe_0'=4,'stripe_1'=4] {'stripe_0'}, use_global_device_ids=true, to_apply=%region_13.14 | all-reduce | flops 2 | bytes 16 | tf_op jit(solution)/shard_map/psum | solution.py:26
  311.8 7.2 %all-reduce = (f32[]{:T(128)}, f32[]{:T(128)}) all-reduce(f32[]{:T(128)} %get-tuple-element.4, f32[]{:T(128)} %get-tuple-element.5), channel_id=1, replica_groups=mesh['rep_0'=4,'rep_1'=2,'rep_2'=2,'stripe_0'=4,'stripe_1'=4] {'stripe_1'}, use_global_device_ids=true, to_apply=%region_14.15 | all-reduce | flops 2 | bytes 16 | tf_op jit(solution)/shard_map/psum | solution.py:26
  321.4 107.2 %all-gather.3.cloned.1.call-done = f32[4096,512]{1,0:T(8,128)} async-done(((f32[256,512]{1,0:T(8,128)}), f32[4096,512]{1,0:T(8,128)}) %all-gather.3.cloned.1.call-update) | async-done | bytes 8388624 | tf_op jit(solution)/shard_map/all_gather | solution.py:100
  428.6 7.7 %gather_fusion.2 = f32[16,256,512]{2,1,0:T(8,128)} fusion(f32[16,256,512]{2,1,0:T(8,128)} %bitcast.41, s32[1024]{0:T(1024)S(1)} %pad_clamp_fusion), kind=kCustom, calls=%fused_computation.2 | custom fusion | bytes 16777280 | tf_op jit(solution)/shard_map/jit(_take)/gather | solution.py:106
  436.3 6.0 %bitcast_select_fusion = f32[4096,512]{1,0:T(8,128)} fusion(f32[16,256,512]{2,1,0:T(8,128)} %gather_fusion.2, pred[4096]{0:T(1024)(128)(4,1)S(1)} %broadcast_in_dim.40), kind=kLoop, calls=%fused_computation.3 | loop fusion | flops 2097152 | bytes 16781312 | tf_op jit(solution)/shard_map/jit(_take)/select_n | solution.py:106
  (32 shorter events, 4.8 us)
Async XLA Ops:
  7.2 11.4 %copy-start = (bf16[256,512]{1,0:T(8,128)(2,1)S(1)}, bf16[256,512]{1,0:T(8,128)(2,1)}, u32[]{:S(2)}) copy-start(bf16[256,512]{1,0:T(8,128)(2,1)} %param.5) | copy-start | bytes 786436
  7.2 169.2 %reduce-scatter.2.cloned.1.call-start = ((), (), s32[]{:S(2)}) async-start(), calls=%async_computation.1 | async-start | bytes 8912896 | tf_op jit(solution)/shard_map/reduce_scatter | solution.py:66
  34.2 394.5 %all-gather.3.cloned.1.call-start = ((), (), s32[]{:S(2)}) async-start(), calls=%async_computation.2 | async-start | bytes 8912896 | tf_op jit(solution)/shard_map/all_gather | solution.py:100
  176.3 12.9 %collective-permute-start = (f32[256,512]{0,1:T(8,128)}, f32[256,512]{0,1:T(8,128)S(1)}, u32[]{:S(2)}, u32[]{:S(2)}) collective-permute-start(f32[256,512]{0,1:T(8,128)} %reduce-scatter.2.cloned.1.call-done), channel_id=1, source_target_pairs={{0,128},{16,144},{32,160},{48,176},{64,192},{80,208},{96,224},{112... | collective-permute-start | bytes 1572872 | tf_op jit(solution)/shard_map/ppermute | solution.py:21
  189.3 1.6 copy-start.3
  196.8 45.2 %copy-start.1 = (f32[512,512]{1,0:T(8,128)}, f32[512,512]{1,0:T(8,128)S(1)}, u32[]{:S(2)}) copy-start(f32[512,512]{1,0:T(8,128)S(1)} %get-tuple-element.13) | copy-start | bytes 3145732
  244.0 1.9 copy-start.2
  252.8 22.3 %collective-permute-start.1 = (f32[512,512]{1,0:T(8,128)S(1)}, f32[512,512]{1,0:T(8,128)S(1)}, u32[]{:S(2)}, u32[]{:S(2)}) collective-permute-start(f32[512,512]{1,0:T(8,128)S(1)} %fusion.47), channel_id=1, source_target_pairs={{0,128},{16,144},{32,160},{48,176},{64,192},{80,208},{96,224},{112... | collective-permute-start | bytes 3145736 | tf_op jit(solution)/shard_map/ppermute | solution.py:21
Sparse Core Ops, SparseCore 0:
  34.3 142.0 reduce-scatter.1
  321.3 107.2 all-gather.2
where the time goes:
time: 450 us; the launch traced here: 449 us
  waiting for transfers between devices  282 us (63%)
  blocking collectives  82.5 us (18%)
  local copies, waits for them, and re-layouts  27.6 us (6%)
  matrix products  27.4 us (6%)
  between operations  16.8 us (4%)
  other arithmetic  10.9 us (2%)
    reduce_scatter x1, waiting for transfers between devices, per_device(): lax.psum_scatter(slot_terms(activations, out_grads, blocks_of, pair_count...  142 us
    all_gather x1, waiting for transfers between devices, per_device(): gathered = lax.all_gather(scaled[None], REP, axis=0, tiled=True)  107 us
    psum x10, blocking collectives, by_axis(): shard = lax.psum(shard, axis)  82.5 us
    ppermute x2, waiting for transfers between devices, partner(): lax.ppermute(shard, axis, [(i, i ^ 1 << stride) for i in range(lax.axis_s...  32.6 us
  transfers between devices with their start and end apart: 4, of which 4 were waited for; matrix products, arithmetic and copies ran while one was open for 0% of the time, Pallas kernels for 0%

commit v1 on v0

v1 whole, which is shorter than its diff:
```python
import functools

import jax
import jax.numpy as jnp
from jax import lax
from jax.experimental import pallas as pl
from jax.experimental.pallas import tpu as pltpu
from jax.sharding import PartitionSpec as P

MESH = pl.DeviceIdType.MESH
f32 = jnp.float32
bf16 = jnp.bfloat16

BLOCK = 512
HALF = 256
DECAY = 0.95
DAMPING = 0.25
EPS = 1e-06
COUNT = 131072.0

RELATIVE = (3, 1, 2, 0)
SEQUENCE = ((0, 2, 1, 3), (1, 2, 0, 3))
QS = 2
ROWS = HALF // 2 // QS
PIECES = 2 * QS


def position():
    rep = lax.axis_index("rep")
    stripe = lax.axis_index("stripe")
    return rep // 4, stripe // 4, (rep // 2) % 2, stripe % 4, rep % 2


def device(x, y, z, c):
    return (x * 4 + (z // 4) * 2 + c, y * 4 + z % 4)


def split(a):
    high = a.astype(bf16)
    low = (a - high.astype(f32)).astype(bf16)
    return high, low


def product(a, b, dims=((1,), (0,))):
    (ah, al), (bh, bl) = a, b

    def dot(u, v):
        return lax.dot_general(u, v, (dims, ((), ())), preferred_element_type=f32)

    return dot(ah, bh) + (dot(ah, bl) + dot(al, bh))


def total(a):
    return jnp.sum(jnp.sum(a, axis=0, keepdims=True), axis=1, keepdims=True)


def eye_mask(n):
    return lax.broadcasted_iota(jnp.int32, (n, n), 0) == lax.broadcasted_iota(jnp.int32, (n, n), 1)


def rows_of(piece):
    return pl.ds(piece * ROWS, ROWS)


def main_kernel(
    blocks, act, og, stat_in,
    gath, new_stat, scale_out,
    acc, psend, precv, ring, zbuf, grad, stat, norm, roots, precond, sums,
    ps_s, ps_r, ring_s, ring_r, z_s, z_r, g_s, g_r, st_s, st_r, ns_s, ns_r, rt_s, rt_r,
    gr_s, gr_r, gz_s, gz_r, gd_s, gd_r, own_s, sum_s, sum_r,
):
    x, y, zh, zl, c = position()
    z = zh * 4 + zl
    sibling = device(x, y, z, 1 - c)
    side = (device((x + 1) % 4, y, z, c), device((x + 3) % 4, y, z, c))
    zmate = device(x, y, (z + 4) % 8, c)
    owner = device((x + 2) % 4, y, z, 1 - c)
    stays = c == x // 2
    moves = c != x // 2

    def remote(src, dst, send, recv, to):
        return pltpu.make_async_remote_copy(
            src_ref=src, dst_ref=dst, send_sem=send, recv_sem=recv, device_id=to, device_id_type=MESH
        )

    groups = (
        [(o, device(((x * 2 + c + o) % 8) // 2, y, z, (x * 2 + c + o) % 2)) for o in range(1, 8)],
        [(o, device(x, (y + o) % 4, z, c)) for o in range(1, 4)],
        [(o, device(x, y, (z + o) % 8, c)) for o in range(1, 8)],
    )
    places = (x * 2 + c, y, z)
    sizes = (8, 4, 8)

    barrier = pltpu.get_barrier_semaphore()
    for group in groups:
        for _, peer in group:
            pl.semaphore_signal(barrier, inc=1, device_id=peer, device_id_type=MESH)
    pl.semaphore_wait(barrier, sum(len(group) for group in groups))

    stat_local = pltpu.make_async_copy(stat_in, stat, own_s.at[0])
    stat_remote = remote(stat_in, stat, st_s, st_r, owner)

    @pl.when(stays)
    def _():
        stat_local.start()

    @pl.when(moves)
    def _():
        stat_remote.start()

    def columns(slot, half):
        xt = (x + RELATIVE[slot % 4]) % 4
        zt = (1 - zh) if slot < 4 else zh
        block = blocks[0, (xt % 2) * 4 + zt * 2 + xt // 2]
        return act[:, pl.ds(block * BLOCK + half * HALF, HALF)]

    def partial(slot, half):
        return lax.dot_general(
            columns(slot, half), og[...], (((0,), (0,)), ((), ())), preferred_element_type=f32
        )

    def ring_copy(phase, d, step, q):
        index = ((phase * 2 + d) * 3 + step) * QS + q
        source = acc.at[phase * 4 + SEQUENCE[d][step], rows_of(d * QS + q)]
        return remote(source, ring.at[index], ring_s.at[index], ring_r.at[index], side[d])

    started = []

    def ring_start(phase, d, step, q):
        copy = ring_copy(phase, d, step, q)
        copy.start()
        started.append(copy)

    def ring_take(phase, d, step, q):
        index = ((phase * 2 + d) * 3 + step) * QS + q
        ring_copy(phase, d, step, q).wait_recv()
        slot = phase * 4 + SEQUENCE[d][step + 1]
        rows = rows_of(d * QS + q)
        acc[slot, rows] = acc[slot, rows] + ring[index]

    def pair_take(slot):
        pair[slot].wait_recv()
        acc[slot] = acc[slot] + precv[slot]

    pair = []
    for slot in range(8):
        psend[slot] = partial(slot, 1 - c)
        copy = remote(psend.at[slot], precv.at[slot], ps_s.at[slot], ps_r.at[slot], sibling)
        copy.start()
        pair.append(copy)
        acc[slot] = partial(slot, c)
        if slot > 0:
            pair_take(slot - 1)
        if slot == 2:
            for q in range(QS):
                for d in range(2):
                    ring_start(0, d, 0, q)
    pair_take(7)

    def advance(phase, step):
        for q in range(QS):
            for d in range(2):
                ring_take(phase, d, step, q)
                ring_start(phase, d, step + 1, q)

    zcopies = [
        remote(acc.at[3, rows_of(i)], zbuf.at[i], z_s.at[i], z_r.at[i], zmate) for i in range(PIECES)
    ]
    advance(0, 0)
    for d in range(2):
        ring_start(1, d, 0, 0)
    advance(0, 1)
    for q in range(1, QS):
        for d in range(2):
            ring_start(1, d, 0, q)
    for q in range(QS):
        for d in range(2):
            ring_take(0, d, 2, q)
            zcopies[d * QS + q].start()
    advance(1, 0)
    advance(1, 1)

    gcopies = []
    for q in range(QS):
        for d in range(2):
            i = d * QS + q
            ring_take(1, d, 2, q)
            zcopies[i].wait_recv()
            here = pl.ds(c * HALF + i * ROWS, ROWS)
            grad[here, :] = acc[7, rows_of(i)] + zbuf[i]
            copy = remote(grad.at[here, :], grad.at[here, :], g_s.at[i], g_r.at[i], sibling)
            copy.start()
            gcopies.append(copy)

    @pl.when(stays)
    def _():
        stat_local.wait()

    @pl.when(moves)
    def _():
        stat_remote.wait()

    lane = lax.broadcasted_iota(jnp.int32, (8, 128), 1)
    sum_copies = []

    def stage_copy(which, stage, o, peer, slot_of):
        base = which * 20 + (0, 8, 12)[stage]
        mine = base + places[stage]
        theirs = base + (places[stage] + o) % sizes[stage]
        send = sum_s.at[base + o]
        return remote(sums.at[mine], sums.at[mine], send, sum_r.at[mine if slot_of == "send" else theirs], peer)

    def stage_start(which, stage, value):
        base = which * 20 + (0, 8, 12)[stage]
        sums[base + places[stage]] = value
        for o, peer in groups[stage]:
            copy = stage_copy(which, stage, o, peer, "send")
            copy.start()
            sum_copies.append(copy)

    def stage_take(which, stage):
        base = which * 20 + (0, 8, 12)[stage]
        for o, peer in groups[stage]:
            stage_copy(which, stage, o, peer, "recv").wait_recv()
        value = sums[base]
        for i in range(1, sizes[stage]):
            value = value + sums[base + i]
        return value

    mask = eye_mask(BLOCK)
    stat_trace = total(jnp.where(mask, stat[...], 0.0))
    half = grad[pl.ds(c * HALF, HALF), :]
    square = total(half * half)
    stage_start(0, 0, jnp.where(lane == 0, stat_trace, 0.0) + jnp.where(lane == 1, square, 0.0))

    for copy in gcopies:
        copy.wait_recv()
    gsplit = split(grad[...])

    @pl.when(c == 0)
    def _():
        stat[...] = DECAY * stat[...] + product(gsplit, gsplit, ((1,), (1,)))

    @pl.when(c == 1)
    def _():
        stat[...] = DECAY * stat[...] + product(gsplit, gsplit, ((0,), (0,)))

    back_local = pltpu.make_async_copy(stat, new_stat, own_s.at[1])
    back_remote = remote(stat, new_stat, ns_s, ns_r, owner)
    value = stage_take(0, 0)
    stage_start(0, 1, value)

    now = stat[...]
    square_sum = total(now * now)
    now_trace = total(jnp.where(mask, now, 0.0))
    size = jnp.sqrt(square_sum + EPS)
    first = now * (1.0 / size)
    norm[0] = first
    first_split = split(first)
    second = product(first_split, first_split)
    norm[1] = second
    value = stage_take(0, 1)
    stage_start(0, 2, value)
    third = product(split(second), first_split)
    norm[2] = third

    @pl.when(stays)
    def _():
        back_local.start()

    @pl.when(moves)
    def _():
        back_remote.start()

    value = stage_take(0, 2)
    top = lax.broadcasted_iota(jnp.int32, (8, 128), 0) == 0
    trace_all = total(jnp.where(top & (lane == 0), value, 0.0))
    grad_sq = total(jnp.where(top & (lane == 1), value, 0.0))
    shift = DAMPING * ((DECAY * trace_all + 2.0 * grad_sq) / COUNT)
    frob = jnp.sqrt(square_sum + (2.0 * shift * now_trace + BLOCK * shift * shift) + EPS)
    ratio = size / frob
    e = shift / frob
    gain = 1.0 / jnp.sqrt(jnp.sqrt(frob))
    a = (
        25.0 / 16.0, -5.0 / 16.0 - 3125.0 / 4096.0, 3125.0 / 4096.0, -1250.0 / 4096.0,
        250.0 / 4096.0, -25.0 / 4096.0, 1.0 / 4096.0,
    )
    binomial = (
        (1,), (1, 1), (1, 2, 1), (1, 3, 3, 1), (1, 4, 6, 4, 1), (1, 5, 10, 10, 5, 1), (1, 6, 15, 20, 15, 6, 1),
    )
    coefs = []
    scale = gain
    for j in range(7):
        coef = jnp.full_like(e, a[6] * binomial[6][j])
        for i in range(5, j - 1, -1):
            coef = coef * e + a[i] * binomial[i][j]
        coefs.append(coef * scale)
        scale = scale * ratio
    first, second, third = norm[0], norm[1], norm[2]
    upper = coefs[4] * first + coefs[5] * second + coefs[6] * third
    root = coefs[1] * first + coefs[2] * second + coefs[3] * third + jnp.where(mask, coefs[0], 0.0)
    root = root + product(split(third), split(upper))
    roots[c] = root
    root_copy = remote(roots.at[c], roots.at[c], rt_s, rt_r, sibling)
    root_copy.start()
    root_copy.wait_recv()

    mine = roots[0, pl.ds(c * HALF, HALF), :]
    left = product(split(mine), gsplit)
    result = product(split(left), split(roots[1]))
    for i in range(PIECES):
        precond[i] = result[i * ROWS : (i + 1) * ROWS]
    stage_start(1, 0, jnp.where(lane == 0, total(result * result), 0.0))

    def place(xt, zt):
        return (xt * 2 + zt) * 2 + c

    gathers = []

    def spread(i, d2d, source, xt, zt):
        where = gath.at[place(xt, zt), rows_of(i)]
        copy = remote(source, where, gd_s.at[d2d], gd_r.at[d2d], sibling)
        copy.start()
        gathers.append(copy)

    def gather_copy(phase, d, step, q):
        index = ((phase * 2 + d) * 3 + step) * QS + q
        xt = (x + 4 - step) % 4 if d == 0 else (x + step) % 4
        zt = zh if phase == 0 else 1 - zh
        where = gath.at[place(xt, zt), rows_of(d * QS + q)]
        source = precond.at[d * QS + q] if phase == 0 and step == 0 else where
        return remote(source, where, gr_s.at[index], gr_r.at[index], side[d])

    def gather_start(phase, d, step, q):
        copy = gather_copy(phase, d, step, q)
        copy.start()
        gathers.append(copy)

    def gather_take(phase, d, step, q):
        gather_copy(phase, d, step, q).wait_recv()
        if step < 2:
            gather_start(phase, d, step + 1, q)
        xt = (x + 3 - step) % 4 if d == 0 else (x + 1 + step) % 4
        zt = zh if phase == 0 else 1 - zh
        spread(d * QS + q, (phase * 4 + step + 1) * PIECES + d * QS + q, gath.at[place(xt, zt), rows_of(d * QS + q)], xt, zt)

    mates = [
        remote(precond.at[i], gath.at[place(x, zh), rows_of(i)], gz_s.at[i], gz_r.at[i], zmate)
        for i in range(PIECES)
    ]
    kept = [
        pltpu.make_async_copy(precond.at[i], gath.at[place(x, zh), rows_of(i)], own_s.at[2 + i])
        for i in range(PIECES)
    ]
    order = [(d, q) for q in range(QS) for d in range(2)]
    for d, q in order:
        mates[d * QS + q].start()
        gather_start(0, d, 0, q)
    for i in range(PIECES):
        spread(i, i, precond.at[i], x, zh)
        kept[i].start()

    def mate_take(d, q):
        i = d * QS + q
        mates[i].wait_recv()
        gather_start(1, d, 0, q)
        spread(i, 4 * PIECES + i, gath.at[place(x, 1 - zh), rows_of(i)], x, 1 - zh)

    for d, q in order:
        gather_take(0, d, 0, q)
    value = stage_take(1, 0)
    stage_start(1, 1, value)
    mate_take(0, 0)
    for d, q in order:
        gather_take(0, d, 1, q)
    value = stage_take(1, 1)
    stage_start(1, 2, value)
    mate_take(1, 0)
    for d, q in order:
        gather_take(0, d, 2, q)
    for q in range(1, QS):
        for d in range(2):
            mate_take(d, q)
    for step in range(3):
        for d, q in order:
            gather_take(1, d, step, q)
    value = stage_take(1, 2)
    prec_sq = total(jnp.where(top & (lane == 0), value, 0.0))
    scale_out[...] = jnp.broadcast_to(jnp.sqrt(grad_sq / (prec_sq + EPS)), (8, 128))

    for i in range(8 * PIECES):
        where = gath.at[0, rows_of(i % PIECES)]
        remote(where, where, gd_s.at[i], gd_r.at[i], sibling).wait_recv()
    for copy in pair + started + zcopies + gcopies + sum_copies + [root_copy] + gathers + mates:
        copy.wait_send()
    for copy in kept:
        copy.wait()

    @pl.when(stays)
    def _():
        back_local.wait()

    @pl.when(moves)
    def _():
        back_remote.wait()


def run_main(blocks, act, og, stat):
    dma = pltpu.SemaphoreType.DMA
    ring_count = 12 * QS
    space = pl.BlockSpec
    return pl.pallas_call(
        main_kernel,
        out_shape=(
            jax.ShapeDtypeStruct((16, HALF, BLOCK), f32),
            jax.ShapeDtypeStruct((BLOCK, BLOCK), f32),
            jax.ShapeDtypeStruct((8, 128), f32),
        ),
        in_specs=[
            space(memory_space=pltpu.SMEM), space(memory_space=pltpu.VMEM),
            space(memory_space=pltpu.VMEM), space(memory_space=pl.ANY),
        ],
        out_specs=(space(memory_space=pl.ANY), space(memory_space=pl.ANY), space(memory_space=pltpu.VMEM)),
        scratch_shapes=[
            pltpu.VMEM((8, HALF, BLOCK), f32),
            pltpu.VMEM((8, HALF, BLOCK), f32),
            pltpu.VMEM((8, HALF, BLOCK), f32),
            pltpu.VMEM((ring_count, ROWS, BLOCK), f32),
            pltpu.VMEM((PIECES, ROWS, BLOCK), f32),
            pltpu.VMEM((BLOCK, BLOCK), f32),
            pltpu.VMEM((BLOCK, BLOCK), f32),
            pltpu.VMEM((3, BLOCK, BLOCK), f32),
            pltpu.VMEM((2, BLOCK, BLOCK), f32),
            pltpu.VMEM((PIECES, ROWS, BLOCK), f32),
            pltpu.VMEM((40, 8, 128), f32),
            dma((8,)), dma((8,)), dma((ring_count,)), dma((ring_count,)), dma((PIECES,)), dma((PIECES,)),
            dma((PIECES,)), dma((PIECES,)), dma(()), dma(()), dma(()), dma(()), dma(()), dma(()),
            dma((ring_count,)), dma((ring_count,)), dma((PIECES,)), dma((PIECES,)),
            dma((8 * PIECES,)), dma((8 * PIECES,)), dma((2 + PIECES,)), dma((40,)), dma((40,)),
        ],
        compiler_params=pltpu.CompilerParams(
            collective_id=0, has_side_effects=True, vmem_limit_bytes=48 * 1024 * 1024
        ),
        name="shampoo",
    )(blocks, act, og, stat)


def place_kernel(order, gath, scale, out):
    out[...] = gath[0] * scale[0:1, 0:1]


def run_place(order, gath, scale):
    return pl.pallas_call(
        place_kernel,
        grid_spec=pltpu.PrefetchScalarGridSpec(
            num_scalar_prefetch=1,
            grid=(16,),
            in_specs=[
                pl.BlockSpec((1, HALF, BLOCK), lambda i, order: (order[i], 0, 0)),
                pl.BlockSpec((8, 128), lambda i, order: (0, 0)),
            ],
            out_specs=pl.BlockSpec((HALF, BLOCK), lambda i, order: (i, 0)),
        ),
        out_shape=jax.ShapeDtypeStruct((16 * HALF, BLOCK), f32),
        name="place",
    )(order, gath, scale)


def per_device(activations, out_grads, statistics, owner_blocks):
    gath, new_stat, scale = run_main(owner_blocks, activations, out_grads, statistics[0, 0])
    pairs = jnp.arange(8, dtype=jnp.int32)
    pair = jnp.sum(pairs[:, None] * (owner_blocks[0][:, None] == pairs[None, :]).astype(jnp.int32), axis=0)
    slot = (pair // 4 + 2 * (pair % 2)) * 2 + (pair // 2) % 2
    order = jnp.stack([slot * 2, slot * 2 + 1], axis=1).reshape(-1)
    return run_place(order, gath, scale), new_stat[None, None]


def solution(mesh):
    return jax.shard_map(
        per_device,
        mesh=mesh,
        in_specs=(P("rep", None), P("rep", "stripe"), P("rep", "stripe", None, None), P("stripe", None)),
        out_specs=(P(None, "stripe"), P("rep", "stripe", None, None)),
        check_vma=False,
    )
```

time: 450 us -> 151 us (0.34)
  waiting for transfers between devices: 282 us -> 0 us
  Pallas kernels: 0 us -> 142 us
  blocking collectives: 82.5 us -> 0 us
  matrix products: 27.4 us -> 0 us
  local copies, waits for them, and re-layouts: 27.6 us -> 6.72 us
  between operations: 16.8 us -> 0.65 us
  other arithmetic: 10.9 us -> 0.78 us
    pallas_call x0 -> x2, Pallas kernels: none -> 142 us  [the longest x1 129 us: run_main(): pl.pallas_call(main_kernel, out_shape=(jax.ShapeDtypeStruct((16, HALF, BL...]
    reduce_scatter x1 -> x0, waiting for transfers between devices: 142 us -> none  [per_device(): lax.psum_scatter(slot_terms(activations, out_grads, blocks_of, pair_count...]
    all_gather x1 -> x0, waiting for transfers between devices: 107 us -> none  [per_device(): gathered = lax.all_gather(scaled[None], REP, axis=0, tiled=True)]
    psum x10 -> x0, blocking collectives: 82.5 us -> none  [by_axis(): shard = lax.psum(shard, axis)]
    ppermute x2 -> x0, waiting for transfers between devices: 32.6 us -> none  [partner(): lax.ppermute(shard, axis, [(i, i ^ 1 << stride) for i in range(lax.axis_s...]
    dot_general x9 -> x0, matrix products: 27.4 us -> none  [the longest x1 6.67 us: slot_terms(): jnp.einsum('tkp,tc->kpc', chosen, out_grads, preferred_element_type=jnp.f...]
    reshape x4 -> x1, local copies, waits for them, and re-layouts: 11.9 us -> 0.66 us  [per_device(): order = jnp.stack([slot * 2, slot * 2 + 1], axis=1).reshape(-1)]
    gather x3 -> x0, local copies, waits for them, and re-layouts: 11 us -> none  [the longest x1 7.67 us: per_device(): jnp.take(gathered, row_order, axis=0)]
  transfers between devices with their start and end apart: 4 -> 0, of which waited for: 4 -> 0; matrix products, arithmetic and copies ran while one was open for 0% -> 0% of each run, Pallas kernels for 0% -> 0%
where the time goes in v1:
time: 151 us; the launch traced here: 150 us
  Pallas kernels  142 us (94%)
  local copies, waits for them, and re-layouts  6.72 us (4%)
    pallas_call x1, Pallas kernels, run_main(): pl.pallas_call(main_kernel, out_shape=(jax.ShapeDtypeStruct((16, HALF, BL...  129 us
    pallas_call x1, Pallas kernels, run_place(): pl.pallas_call(place_kernel, grid_spec=pltpu.PrefetchScalarGridSpec(num_s...  12.8 us
    unnamed x11, local copies, waits for them, and re-layouts  5.98 us

profile of v1, /device:TPU:1, one launch (start us, length us, event | category | flops | bytes accessed | tf_op | source)
XLA Modules:
  0.0 150.5 jit_solution(14449525193764843247)
XLA Ops:
  0.6 0.7 select_reduce_fusion
  1.4 0.1 copy.8
  1.5 0.7 reshape.161.order
  2.1 0.0 copy-start
  2.2 1.6 %copy-done = bf16[256,4096]{1,0:T(8,128)(2,1)S(1)} copy-done((bf16[256,4096]{1,0:T(8,128)(2,1)S(1)}, bf16[256,4096]{1,0:T(8,128)(2,1)}, u32[]{:S(2)}) %copy-start) | copy-done | bytes 2097176
  3.7 0.0 copy-start.1
  3.7 1.2 copy-done.1
  5.0 0.0 copy-start.2
  5.0 0.9 copy-done.2
  5.9 0.0 copy-start.4
  5.9 0.7 copy-done.4
  6.6 129.5 %shampoo.1 = (f32[16,256,512]{2,1,0:T(8,128)}, f32[512,512]{1,0:T(8,128)S(1)}, f32[8,128]{1,0:T(8,128)S(1)}) custom-call(s32[1,8]{1,0:T(1,128)S(1)} %copy-done.4, bf16[256,4096]{1,0:T(8,128)(2,1)S(1)} %copy-done, bf16[256,512]{1,0:T(8,128)(2,1)S(1)} %copy-done.2, f32[512,512]{1,0:T(8,128)S(1)} %bitcast.23), custom_call_target="tpu_custom_call" | custom-call | tf_op jit(solution)/shard_map/shampoo/pallas_call | solution.py:412
  136.0 0.0 copy-start.3
  136.1 0.6 copy-done.3
  136.6 12.8 %place.1 = f32[4096,512]{1,0:T(8,128)} custom-call(s32[16]{0:T(128)} %reshape.161.order, f32[16,256,512]{2,1,0:T(8,128)} %get-tuple-element.5.gath, f32[8,128]{1,0:T(8,128)} %copy-done.3), custom_call_target="tpu_custom_call" | custom-call | tf_op jit(solution)/shard_map/place/pallas_call | solution.py:453
  149.5 1.0 copy.10
  (2 shorter events, 0.0 us)
Async XLA Ops:
  2.1 1.6 %copy-start = (bf16[256,4096]{1,0:T(8,128)(2,1)S(1)}, bf16[256,4096]{1,0:T(8,128)(2,1)}, u32[]{:S(2)}) copy-start(bf16[256,4096]{1,0:T(8,128)(2,1)} %act.1) | copy-start | bytes 6291460
  3.7 1.2 copy-start.1
  5.0 0.9 copy-start.2
  5.9 0.7 copy-start.4
  136.0 0.6 copy-start.3

commit v2 on v1

--- a/solution.py
+++ b/solution.py
@@ -63,11 +63,11 @@
 
 
 def main_kernel(
-    blocks, act, og, stat_in,
+    blocks, act_in, og_in, stat_in,
     gath, new_stat, scale_out,
-    acc, psend, precv, ring, zbuf, grad, stat, norm, roots, precond, sums,
+    act, og, acc, psend, precv, ring, zbuf, grad, stat, norm, roots, precond, sums,
     ps_s, ps_r, ring_s, ring_r, z_s, z_r, g_s, g_r, st_s, st_r, ns_s, ns_r, rt_s, rt_r,
-    gr_s, gr_r, gz_s, gz_r, gd_s, gd_r, own_s, sum_s, sum_r,
+    gr_s, gr_r, gz_s, gz_r, gd_s, gd_r, own_s, sum_s, sum_r, in_s,
 ):
     x, y, zh, zl, c = position()
     z = zh * 4 + zl
@@ -91,6 +91,9 @@
     places = (x * 2 + c, y, z)
     sizes = (8, 4, 8)
 
+    inputs = [pltpu.make_async_copy(act_in, act, in_s.at[0]), pltpu.make_async_copy(og_in, og, in_s.at[1])]
+    for copy in inputs:
+        copy.start()
     barrier = pltpu.get_barrier_semaphore()
     for group in groups:
         for _, peer in group:
@@ -142,6 +145,8 @@
         pair[slot].wait_recv()
         acc[slot] = acc[slot] + precv[slot]
 
+    for copy in inputs:
+        copy.wait()
     pair = []
     for slot in range(8):
         psend[slot] = partial(slot, 1 - c)
@@ -245,7 +250,6 @@
     def _():
         stat[...] = DECAY * stat[...] + product(gsplit, gsplit, ((0,), (0,)))
 
-    back_local = pltpu.make_async_copy(stat, new_stat, own_s.at[1])
     back_remote = remote(stat, new_stat, ns_s, ns_r, owner)
     value = stage_take(0, 0)
     stage_start(0, 1, value)
@@ -266,7 +270,7 @@
 
     @pl.when(stays)
     def _():
-        back_local.start()
+        new_stat[...] = stat[...]
 
     @pl.when(moves)
     def _():
@@ -348,17 +352,13 @@
         remote(precond.at[i], gath.at[place(x, zh), rows_of(i)], gz_s.at[i], gz_r.at[i], zmate)
         for i in range(PIECES)
     ]
-    kept = [
-        pltpu.make_async_copy(precond.at[i], gath.at[place(x, zh), rows_of(i)], own_s.at[2 + i])
-        for i in range(PIECES)
-    ]
     order = [(d, q) for q in range(QS) for d in range(2)]
     for d, q in order:
         mates[d * QS + q].start()
         gather_start(0, d, 0, q)
     for i in range(PIECES):
         spread(i, i, precond.at[i], x, zh)
-        kept[i].start()
+        gath[place(x, zh), rows_of(i)] = precond[i]
 
     def mate_take(d, q):
         i = d * QS + q
@@ -393,12 +393,6 @@
         remote(where, where, gd_s.at[i], gd_r.at[i], sibling).wait_recv()
     for copy in pair + started + zcopies + gcopies + sum_copies + [root_copy] + gathers + mates:
         copy.wait_send()
-    for copy in kept:
-        copy.wait()
-
-    @pl.when(stays)
-    def _():
-        back_local.wait()
 
     @pl.when(moves)
     def _():
@@ -417,11 +411,13 @@
             jax.ShapeDtypeStruct((8, 128), f32),
         ),
         in_specs=[
-            space(memory_space=pltpu.SMEM), space(memory_space=pltpu.VMEM),
-            space(memory_space=pltpu.VMEM), space(memory_space=pl.ANY),
+            space(memory_space=pltpu.SMEM), space(memory_space=pltpu.HBM),
+            space(memory_space=pltpu.HBM), space(memory_space=pltpu.HBM),
         ],
-        out_specs=(space(memory_space=pl.ANY), space(memory_space=pl.ANY), space(memory_space=pltpu.VMEM)),
+        out_specs=(space(memory_space=pltpu.VMEM), space(memory_space=pltpu.VMEM), space(memory_space=pltpu.VMEM)),
         scratch_shapes=[
+            pltpu.VMEM((HALF, 4096), bf16),
+            pltpu.VMEM((HALF, BLOCK), bf16),
             pltpu.VMEM((8, HALF, BLOCK), f32),
             pltpu.VMEM((8, HALF, BLOCK), f32),
             pltpu.VMEM((8, HALF, BLOCK), f32),
@@ -436,43 +432,56 @@
             dma((8,)), dma((8,)), dma((ring_count,)), dma((ring_count,)), dma((PIECES,)), dma((PIECES,)),
             dma((PIECES,)), dma((PIECES,)), dma(()), dma(()), dma(()), dma(()), dma(()), dma(()),
             dma((ring_count,)), dma((ring_count,)), dma((PIECES,)), dma((PIECES,)),
-            dma((8 * PIECES,)), dma((8 * PIECES,)), dma((2 + PIECES,)), dma((40,)), dma((40,)),
+            dma((8 * PIECES,)), dma((8 * PIECES,)), dma((2 + PIECES,)), dma((40,)), dma((40,)), dma((2,)),
         ],
         compiler_params=pltpu.CompilerParams(
-            collective_id=0, has_side_effects=True, vmem_limit_bytes=48 * 1024 * 1024
+            collective_id=0, has_side_effects=True, vmem_limit_bytes=40 * 1024 * 1024
         ),
         name="shampoo",
     )(blocks, act, og, stat)
 
 
-def place_kernel(order, gath, scale, out):
-    out[...] = gath[0] * scale[0:1, 0:1]
-
-
-def run_place(order, gath, scale):
+def place_kernel(blocks, gath, stat_in, scale, out, stat_out, stage, sem):
+    stat_copy = pltpu.make_async_copy(stat_in, stat_out, sem.at[8])
+    stat_copy.start()
+    copies = []
+    for block in range(8):
+        pair = jnp.int32(0)
+        for p in range(1, 8):
+            pair = jnp.where(blocks[0, p] == block, p, pair)
+        slot = (pair // 4 + 2 * (pair % 2)) * 2 + (pair // 2) % 2
+        for half in range(2):
+            stage[block, half * HALF : (half + 1) * HALF] = gath[slot * 2 + half] * scale[0:1, 0:1]
+        copy = pltpu.make_async_copy(stage.at[block], out.at[pl.ds(block * BLOCK, BLOCK)], sem.at[block])
+        copy.start()
+        copies.append(copy)
+    for copy in copies:
+        copy.wait()
+    stat_copy.wait()
+
+
+def run_place(blocks, gath, stat, scale):
+    vmem = pl.BlockSpec(memory_space=pltpu.VMEM)
+    hbm = pl.BlockSpec(memory_space=pltpu.HBM)
     return pl.pallas_call(
         place_kernel,
-        grid_spec=pltpu.PrefetchScalarGridSpec(
-            num_scalar_prefetch=1,
-            grid=(16,),
-            in_specs=[
-                pl.BlockSpec((1, HALF, BLOCK), lambda i, order: (order[i], 0, 0)),
-                pl.BlockSpec((8, 128), lambda i, order: (0, 0)),
-            ],
-            out_specs=pl.BlockSpec((HALF, BLOCK), lambda i, order: (i, 0)),
+        in_specs=[pl.BlockSpec(memory_space=pltpu.SMEM), vmem, vmem, vmem],
+        out_specs=(hbm, hbm),
+        out_shape=(
+            jax.ShapeDtypeStruct((8 * BLOCK, BLOCK), f32),
+            jax.ShapeDtypeStruct((BLOCK, BLOCK), f32),
         ),
-        out_shape=jax.ShapeDtypeStruct((16 * HALF, BLOCK), f32),
+        scratch_shapes=[pltpu.VMEM((8, BLOCK, BLOCK), f32), pltpu.SemaphoreType.DMA((9,))],
+        compiler_params=pltpu.CompilerParams(vmem_limit_bytes=24 * 1024 * 1024),
         name="place",
-    )(order, gath, scale)
+    )(blocks, gath, stat, scale)
 
 
 def per_device(activations, out_grads, statistics, owner_blocks):
-    gath, new_stat, scale = run_main(owner_blocks, activations, out_grads, statistics[0, 0])
-    pairs = jnp.arange(8, dtype=jnp.int32)
-    pair = jnp.sum(pairs[:, None] * (owner_blocks[0][:, None] == pairs[None, :]).astype(jnp.int32), axis=0)
-    slot = (pair // 4 + 2 * (pair % 2)) * 2 + (pair // 2) % 2
-    order = jnp.stack([slot * 2, slot * 2 + 1], axis=1).reshape(-1)
-    return run_place(order, gath, scale), new_stat[None, None]
+    held = [pltpu.with_memory_space_constraint(a, pltpu.HBM) for a in (owner_blocks, activations, out_grads, statistics[0, 0])]
+    gath, new_stat, scale = run_main(*held)
+    rows, new_stat = run_place(held[0], gath, new_stat, scale)
+    return rows, new_stat[None, None]
 
 
 def solution(mesh):

time: 151 us -> 135 us (0.89)
  Pallas kernels: 142 us -> 134 us
  local copies, waits for them, and re-layouts: 6.72 us -> 0 us
    pallas_call x1, Pallas kernels: 12.8 us -> 4.4 us  [run_place(): pl.pallas_call(place_kernel, in_specs=[pl.BlockSpec(memory_space=pltpu.SM...]
    unnamed x11 -> x0, local copies, waits for them, and re-layouts: 5.98 us -> none
where the time goes in v2:
time: 135 us; the launch traced here: 134 us
  Pallas kernels  134 us (99%)
    pallas_call x1, Pallas kernels, run_main(): pl.pallas_call(main_kernel, out_shape=(jax.ShapeDtypeStruct((16, HALF, BL...  129 us
    pallas_call x1, Pallas kernels, run_place(): pl.pallas_call(place_kernel, in_specs=[pl.BlockSpec(memory_space=pltpu.SM...  4.4 us

profile of v2, /device:TPU:1, one launch (start us, length us, event | category | flops | bytes accessed | tf_op | source)
XLA Modules:
  0.0 134.4 jit_solution(8882895088716984125)
XLA Ops:
  0.6 129.4 %shampoo.1 = (f32[16,256,512]{2,1,0:T(8,128)S(1)}, f32[512,512]{1,0:T(8,128)S(1)}, f32[8,128]{1,0:T(8,128)S(1)}) custom-call(s32[1,8]{1,0:T(1,128)} %blocks.3, bf16[256,4096]{1,0:T(8,128)(2,1)} %act_in.1, bf16[256,512]{1,0:T(8,128)(2,1)} %og_in.1, f32[512,512]{1,0:T(8,128)} %bitcast.2), custom_call_target="tpu_custom_call" | custom-call | tf_op jit(solution)/shard_map/shampoo/pallas_call | solution.py:406
  130.0 4.4 %place.1 = (f32[4096,512]{1,0:T(8,128)}, f32[512,512]{1,0:T(8,128)}) custom-call(s32[1,8]{1,0:T(1,128)} %blocks.3, f32[16,256,512]{2,1,0:T(8,128)S(1)} %get-tuple-element.7.gath, f32[512,512]{1,0:T(8,128)S(1)} %get-tuple-element.8.stat_in, f32[8,128]{1,0:T(8,128)S(1)} %get-tuple-element.9.scale), custom_call_target="tpu_custom_call" | custom-call | tf_op jit(solution)/shard_map/place/pallas_call | solution.py:466

commit v3 on v2

--- a/solution.py
+++ b/solution.py
@@ -13,6 +13,7 @@
 
 BLOCK = 512
 HALF = 256
+TILE = 128
 DECAY = 0.95
 DAMPING = 0.25
 EPS = 1e-06
@@ -65,7 +66,7 @@
 def main_kernel(
     blocks, act_in, og_in, stat_in,
     gath, new_stat, scale_out,
-    act, og, acc, psend, precv, ring, zbuf, grad, stat, norm, roots, precond, sums,
+    act, og, diag, acc, psend, precv, ring, zbuf, grad, stat, norm, roots, precond, sums,
     ps_s, ps_r, ring_s, ring_r, z_s, z_r, g_s, g_r, st_s, st_r, ns_s, ns_r, rt_s, rt_r,
     gr_s, gr_r, gz_s, gz_r, gd_s, gd_r, own_s, sum_s, sum_r, in_s,
 ):
@@ -84,14 +85,17 @@
         )
 
     groups = (
+        [(o, device(x, y, (z + o) % 8, c)) for o in range(1, 8)],
+        [(o, device(x, (y + o) % 4, z, c)) for o in range(1, 4)],
         [(o, device(((x * 2 + c + o) % 8) // 2, y, z, (x * 2 + c + o) % 2)) for o in range(1, 8)],
-        [(o, device(x, (y + o) % 4, z, c)) for o in range(1, 4)],
-        [(o, device(x, y, (z + o) % 8, c)) for o in range(1, 8)],
     )
-    places = (x * 2 + c, y, z)
+    places = (z, y, x * 2 + c)
     sizes = (8, 4, 8)
 
     inputs = [pltpu.make_async_copy(act_in, act, in_s.at[0]), pltpu.make_async_copy(og_in, og, in_s.at[1])]
+    for i in range(4):
+        tile = pl.ds(i * TILE, TILE)
+        inputs.append(pltpu.make_async_copy(stat_in.at[tile, tile], diag.at[i], in_s.at[2 + i]))
     for copy in inputs:
         copy.start()
     barrier = pltpu.get_barrier_semaphore()
@@ -100,16 +104,23 @@
             pl.semaphore_signal(barrier, inc=1, device_id=peer, device_id_type=MESH)
     pl.semaphore_wait(barrier, sum(len(group) for group in groups))
 
-    stat_local = pltpu.make_async_copy(stat_in, stat, own_s.at[0])
-    stat_remote = remote(stat_in, stat, st_s, st_r, owner)
+    stat_local = pltpu.make_async_copy(stat_in, stat, own_s)
+    stat_remote = []
+    back_remote = []
+    for i in range(4):
+        rows, cols = pl.ds(i * TILE, TILE), pl.ds(i * TILE, BLOCK - i * TILE)
+        stat_remote.append(remote(stat_in.at[rows, cols], stat.at[rows, cols], st_s.at[i], st_r.at[i], owner))
+        back_remote.append(remote(stat.at[rows, cols], new_stat.at[rows, cols], ns_s.at[i], ns_r.at[i], owner))
+
+    def mirror(ref):
+        for i in range(4):
+            for j in range(i + 1, 4):
+                a, b = slice(i * TILE, (i + 1) * TILE), slice(j * TILE, (j + 1) * TILE)
+                ref[b, a] = ref[a, b].T
 
     @pl.when(stays)
     def _():
         stat_local.start()
-
-    @pl.when(moves)
-    def _():
-        stat_remote.start()
 
     def columns(slot, half):
         xt = (x + RELATIVE[slot % 4]) % 4
@@ -185,6 +196,11 @@
     advance(1, 0)
     advance(1, 1)
 
+    @pl.when(moves)
+    def _():
+        for copy in stat_remote:
+            copy.start()
+
     gcopies = []
     for q in range(QS):
         for d in range(2):
@@ -197,14 +213,6 @@
             copy.start()
             gcopies.append(copy)
 
-    @pl.when(stays)
-    def _():
-        stat_local.wait()
-
-    @pl.when(moves)
-    def _():
-        stat_remote.wait()
-
     lane = lax.broadcasted_iota(jnp.int32, (8, 128), 1)
     sum_copies = []
 
@@ -233,7 +241,8 @@
         return value
 
     mask = eye_mask(BLOCK)
-    stat_trace = total(jnp.where(mask, stat[...], 0.0))
+    diagonal = diag[0] + diag[1] + diag[2] + diag[3]
+    stat_trace = total(jnp.where(eye_mask(TILE), diagonal, 0.0))
     half = grad[pl.ds(c * HALF, HALF), :]
     square = total(half * half)
     stage_start(0, 0, jnp.where(lane == 0, stat_trace, 0.0) + jnp.where(lane == 1, square, 0.0))
@@ -244,17 +253,29 @@
 
     @pl.when(c == 0)
     def _():
-        stat[...] = DECAY * stat[...] + product(gsplit, gsplit, ((1,), (1,)))
+        norm[0] = product(gsplit, gsplit, ((1,), (1,)))
 
     @pl.when(c == 1)
     def _():
-        stat[...] = DECAY * stat[...] + product(gsplit, gsplit, ((0,), (0,)))
-
-    back_remote = remote(stat, new_stat, ns_s, ns_r, owner)
+        norm[0] = product(gsplit, gsplit, ((0,), (0,)))
+
     value = stage_take(0, 0)
     stage_start(0, 1, value)
 
-    now = stat[...]
+    @pl.when(stays)
+    def _():
+        stat_local.wait()
+
+    @pl.when(moves)
+    def _():
+        for copy in stat_remote:
+            copy.wait()
+        mirror(stat)
+
+    now = DECAY * stat[...] + norm[0]
+    stat[...] = now
+    value = stage_take(0, 1)
+    stage_start(0, 2, value)
     square_sum = total(now * now)
     now_trace = total(jnp.where(mask, now, 0.0))
     size = jnp.sqrt(square_sum + EPS)
@@ -263,20 +284,20 @@
     first_split = split(first)
     second = product(first_split, first_split)
     norm[1] = second
-    value = stage_take(0, 1)
-    stage_start(0, 2, value)
     third = product(split(second), first_split)
     norm[2] = third
 
+    value = stage_take(0, 2)
+
     @pl.when(stays)
     def _():
         new_stat[...] = stat[...]
 
     @pl.when(moves)
     def _():
-        back_remote.start()
-
-    value = stage_take(0, 2)
+        for copy in back_remote:
+            copy.start()
+
     top = lax.broadcasted_iota(jnp.int32, (8, 128), 0) == 0
     trace_all = total(jnp.where(top & (lane == 0), value, 0.0))
     grad_sq = total(jnp.where(top & (lane == 1), value, 0.0))
@@ -381,6 +402,13 @@
     for q in range(1, QS):
         for d in range(2):
             mate_take(d, q)
+
+    @pl.when(moves)
+    def _():
+        for copy in back_remote:
+            copy.wait()
+        mirror(new_stat)
+
     for step in range(3):
         for d, q in order:
             gather_take(1, d, step, q)
@@ -393,10 +421,6 @@
         remote(where, where, gd_s.at[i], gd_r.at[i], sibling).wait_recv()
     for copy in pair + started + zcopies + gcopies + sum_copies + [root_copy] + gathers + mates:
         copy.wait_send()
-
-    @pl.when(moves)
-    def _():
-        back_remote.wait()
 
 
 def run_main(blocks, act, og, stat):
@@ -418,6 +442,7 @@
         scratch_shapes=[
             pltpu.VMEM((HALF, 4096), bf16),
             pltpu.VMEM((HALF, BLOCK), bf16),
+            pltpu.VMEM((4, TILE, TILE), f32),
             pltpu.VMEM((8, HALF, BLOCK), f32),
             pltpu.VMEM((8, HALF, BLOCK), f32),
             pltpu.VMEM((8, HALF, BLOCK), f32),
@@ -430,9 +455,9 @@
             pltpu.VMEM((PIECES, ROWS, BLOCK), f32),
             pltpu.VMEM((40, 8, 128), f32),
             dma((8,)), dma((8,)), dma((ring_count,)), dma((ring_count,)), dma((PIECES,)), dma((PIECES,)),
-            dma((PIECES,)), dma((PIECES,)), dma(()), dma(()), dma(()), dma(()), dma(()), dma(()),
+            dma((PIECES,)), dma((PIECES,)), dma((4,)), dma((4,)), dma((4,)), dma((4,)), dma(()), dma(()),
             dma((ring_count,)), dma((ring_count,)), dma((PIECES,)), dma((PIECES,)),
-            dma((8 * PIECES,)), dma((8 * PIECES,)), dma((2 + PIECES,)), dma((40,)), dma((40,)), dma((2,)),
+            dma((8 * PIECES,)), dma((8 * PIECES,)), dma(()), dma((40,)), dma((40,)), dma((6,)),
         ],
         compiler_params=pltpu.CompilerParams(
             collective_id=0, has_side_effects=True, vmem_limit_bytes=40 * 1024 * 1024

time: 135 us -> 128 us (0.948)
  the two profiles are of different devices: /device:TPU:1 before, /device:TPU:33 now
where the time goes in v3:
time: 128 us
  Pallas kernels  127 us (99%)
    pallas_call x1, Pallas kernels, run_main(): pl.pallas_call(main_kernel, out_shape=(jax.ShapeDtypeStruct((16, HALF, BL...  123 us
    pallas_call x1, Pallas kernels, run_place(): pl.pallas_call(place_kernel, in_specs=[pl.BlockSpec(memory_space=pltpu.SM...  4.4 us

profile of v3, /device:TPU:33, one launch (start us, length us, event | category | flops | bytes accessed | tf_op | source)
XLA Modules:
  0.0 128.1 jit_solution(13246399143707503453)
XLA Ops:
  0.6 123.1 %shampoo.1 = (f32[16,256,512]{2,1,0:T(8,128)S(1)}, f32[512,512]{1,0:T(8,128)S(1)}, f32[8,128]{1,0:T(8,128)S(1)}) custom-call(s32[1,8]{1,0:T(1,128)} %blocks.3, bf16[256,4096]{1,0:T(8,128)(2,1)} %act_in.1, bf16[256,512]{1,0:T(8,128)(2,1)} %og_in.1, f32[512,512]{1,0:T(8,128)} %bitcast.2), custom_call_target="tpu_custom_call" | custom-call | tf_op jit(solution)/shard_map/shampoo/pallas_call | solution.py:430
  123.7 4.4 %place.1 = (f32[4096,512]{1,0:T(8,128)}, f32[512,512]{1,0:T(8,128)}) custom-call(s32[1,8]{1,0:T(1,128)} %blocks.3, f32[16,256,512]{2,1,0:T(8,128)S(1)} %get-tuple-element.7.gath, f32[512,512]{1,0:T(8,128)S(1)} %get-tuple-element.8.stat_in, f32[8,128]{1,0:T(8,128)S(1)} %get-tuple-element.9.scale), custom_call_target="tpu_custom_call" | custom-call | tf_op jit(solution)/shard_map/place/pallas_call | solution.py:491

commit v4 on v3

--- a/solution.py
+++ b/solution.py
@@ -21,9 +21,10 @@
 
 RELATIVE = (3, 1, 2, 0)
 SEQUENCE = ((0, 2, 1, 3), (1, 2, 0, 3))
-QS = 2
+QS = 4
 ROWS = HALF // 2 // QS
 PIECES = 2 * QS
+PAIR, RING, ZX, GRAD, ST, NS, SUMS, ROOT, GRING, GZ, SPREAD = range(11)
 
 
 def position():
@@ -67,8 +68,7 @@
     blocks, act_in, og_in, stat_in,
     gath, new_stat, scale_out,
     act, og, diag, acc, psend, precv, ring, zbuf, grad, stat, norm, roots, precond, sums,
-    ps_s, ps_r, ring_s, ring_r, z_s, z_r, g_s, g_r, st_s, st_r, ns_s, ns_r, rt_s, rt_r,
-    gr_s, gr_r, gz_s, gz_r, gd_s, gd_r, own_s, sum_s, sum_r, in_s,
+    send, pair_r, ring_r, z_r, one_r, sum_r, own_s, in_s,
 ):
     x, y, zh, zl, c = position()
     z = zh * 4 + zl
@@ -79,10 +79,16 @@
     stays = c == x // 2
     moves = c != x // 2
 
-    def remote(src, dst, send, recv, to):
+    def remote(src, dst, kind, recv, to):
         return pltpu.make_async_remote_copy(
-            src_ref=src, dst_ref=dst, send_sem=send, recv_sem=recv, device_id=to, device_id_type=MESH
+            src_ref=src, dst_ref=dst, send_sem=send.at[kind], recv_sem=recv, device_id=to, device_id_type=MESH
         )
+
+    def sent(kind, size):
+        remote(size, size, kind, one_r.at[0], sibling).wait_send()
+
+    def received(recv, size):
+        remote(size, size, 0, recv, sibling).wait_recv()
 
     groups = (
         [(o, device(x, y, (z + o) % 8, c)) for o in range(1, 8)],
@@ -109,8 +115,10 @@
     back_remote = []
     for i in range(4):
         rows, cols = pl.ds(i * TILE, TILE), pl.ds(i * TILE, BLOCK - i * TILE)
-        stat_remote.append(remote(stat_in.at[rows, cols], stat.at[rows, cols], st_s.at[i], st_r.at[i], owner))
-        back_remote.append(remote(stat.at[rows, cols], new_stat.at[rows, cols], ns_s.at[i], ns_r.at[i], owner))
+        stat_remote.append(remote(stat_in.at[rows, cols], stat.at[rows, cols], ST, one_r.at[0], owner))
+        back_remote.append(remote(stat.at[rows, cols], new_stat.at[rows, cols], NS, one_r.at[1], owner))
+
+    triangle = ring.at[pl.ds(0, (BLOCK + 3 * TILE + 2 * TILE + TILE) * TILE // (ROWS * BLOCK))]
 
     def mirror(ref):
         for i in range(4):
@@ -136,14 +144,10 @@
     def ring_copy(phase, d, step, q):
         index = ((phase * 2 + d) * 3 + step) * QS + q
         source = acc.at[phase * 4 + SEQUENCE[d][step], rows_of(d * QS + q)]
-        return remote(source, ring.at[index], ring_s.at[index], ring_r.at[index], side[d])
-
-    started = []
+        return remote(source, ring.at[index], RING, ring_r.at[index], side[d])
 
     def ring_start(phase, d, step, q):
-        copy = ring_copy(phase, d, step, q)
-        copy.start()
-        started.append(copy)
+        ring_copy(phase, d, step, q).start()
 
     def ring_take(phase, d, step, q):
         index = ((phase * 2 + d) * 3 + step) * QS + q
@@ -159,49 +163,62 @@
     for copy in inputs:
         copy.wait()
     pair = []
-    for slot in range(8):
+
+    def pair_start(slot):
         psend[slot] = partial(slot, 1 - c)
-        copy = remote(psend.at[slot], precv.at[slot], ps_s.at[slot], ps_r.at[slot], sibling)
+        copy = remote(psend.at[slot], precv.at[slot], PAIR, pair_r.at[slot], sibling)
         copy.start()
         pair.append(copy)
+
+    def make(slot):
+        pair_start(slot)
         acc[slot] = partial(slot, c)
-        if slot > 0:
-            pair_take(slot - 1)
-        if slot == 2:
-            for q in range(QS):
-                for d in range(2):
-                    ring_start(0, d, 0, q)
-    pair_take(7)
-
-    def advance(phase, step):
-        for q in range(QS):
+
+    def advance(phase, step, qs):
+        for q in qs:
             for d in range(2):
                 ring_take(phase, d, step, q)
                 ring_start(phase, d, step + 1, q)
 
-    zcopies = [
-        remote(acc.at[3, rows_of(i)], zbuf.at[i], z_s.at[i], z_r.at[i], zmate) for i in range(PIECES)
-    ]
-    advance(0, 0)
-    for d in range(2):
-        ring_start(1, d, 0, 0)
-    advance(0, 1)
-    for q in range(1, QS):
+    zcopies = [remote(acc.at[3, rows_of(i)], zbuf.at[i], ZX, z_r.at[i], zmate) for i in range(PIECES)]
+    pair_start(0)
+    pair_start(1)
+    for slot in range(2):
+        acc[slot] = partial(slot, c)
+        pair_take(slot)
+        for q in range(QS):
+            ring_start(0, slot, 0, q)
+    make(2)
+    make(3)
+    pair_take(2)
+    advance(0, 0, (0, 1))
+    make(4)
+    pair_take(3)
+    advance(0, 0, (2, 3))
+    make(5)
+    pair_take(4)
+    advance(0, 1, (0, 1))
+    make(6)
+    pair_take(5)
+    advance(0, 1, (2, 3))
+    for q in range(QS):
         for d in range(2):
             ring_start(1, d, 0, q)
+    make(7)
+    pair_take(6)
     for q in range(QS):
         for d in range(2):
             ring_take(0, d, 2, q)
             zcopies[d * QS + q].start()
-    advance(1, 0)
-    advance(1, 1)
+    pair_take(7)
+    advance(1, 0, range(4))
+    advance(1, 1, range(4))
 
     @pl.when(moves)
     def _():
         for copy in stat_remote:
             copy.start()
 
-    gcopies = []
     for q in range(QS):
         for d in range(2):
             i = d * QS + q
@@ -209,32 +226,20 @@
             zcopies[i].wait_recv()
             here = pl.ds(c * HALF + i * ROWS, ROWS)
             grad[here, :] = acc[7, rows_of(i)] + zbuf[i]
-            copy = remote(grad.at[here, :], grad.at[here, :], g_s.at[i], g_r.at[i], sibling)
-            copy.start()
-            gcopies.append(copy)
+            remote(grad.at[here, :], grad.at[here, :], GRAD, one_r.at[2], sibling).start()
 
     lane = lax.broadcasted_iota(jnp.int32, (8, 128), 1)
-    sum_copies = []
-
-    def stage_copy(which, stage, o, peer, slot_of):
+
+    def stage_start(which, stage, value):
         base = which * 20 + (0, 8, 12)[stage]
         mine = base + places[stage]
-        theirs = base + (places[stage] + o) % sizes[stage]
-        send = sum_s.at[base + o]
-        return remote(sums.at[mine], sums.at[mine], send, sum_r.at[mine if slot_of == "send" else theirs], peer)
-
-    def stage_start(which, stage, value):
-        base = which * 20 + (0, 8, 12)[stage]
-        sums[base + places[stage]] = value
-        for o, peer in groups[stage]:
-            copy = stage_copy(which, stage, o, peer, "send")
-            copy.start()
-            sum_copies.append(copy)
+        sums[mine] = value
+        for _, peer in groups[stage]:
+            remote(sums.at[mine], sums.at[mine], SUMS, sum_r.at[which * 3 + stage], peer).start()
 
     def stage_take(which, stage):
         base = which * 20 + (0, 8, 12)[stage]
-        for o, peer in groups[stage]:
-            stage_copy(which, stage, o, peer, "recv").wait_recv()
+        received(sum_r.at[which * 3 + stage], sums.at[pl.ds(base, sizes[stage] - 1)])
         value = sums[base]
         for i in range(1, sizes[stage]):
             value = value + sums[base + i]
@@ -247,8 +252,7 @@
     square = total(half * half)
     stage_start(0, 0, jnp.where(lane == 0, stat_trace, 0.0) + jnp.where(lane == 1, square, 0.0))
 
-    for copy in gcopies:
-        copy.wait_recv()
+    received(one_r.at[2], grad.at[pl.ds(0, HALF), :])
     gsplit = split(grad[...])
 
     @pl.when(c == 0)
@@ -268,8 +272,7 @@
 
     @pl.when(moves)
     def _():
-        for copy in stat_remote:
-            copy.wait()
+        received(one_r.at[0], triangle)
         mirror(stat)
 
     now = DECAY * stat[...] + norm[0]
@@ -323,15 +326,16 @@
         scale = scale * ratio
     first, second, third = norm[0], norm[1], norm[2]
     upper = coefs[4] * first + coefs[5] * second + coefs[6] * third
-    root = coefs[1] * first + coefs[2] * second + coefs[3] * third + jnp.where(mask, coefs[0], 0.0)
-    root = root + product(split(third), split(upper))
-    roots[c] = root
-    root_copy = remote(roots.at[c], roots.at[c], rt_s, rt_r, sibling)
-    root_copy.start()
-    root_copy.wait_recv()
-
-    mine = roots[0, pl.ds(c * HALF, HALF), :]
-    left = product(split(mine), gsplit)
+    upper = split(upper)
+    low = coefs[1] * first + coefs[2] * second + coefs[3] * third + jnp.where(mask, coefs[0], 0.0)
+    for half in (1, 0):
+        rows = slice(half * HALF, (half + 1) * HALF)
+        roots[c, rows] = low[rows] + product(split(third[rows]), upper)
+        part = roots.at[c, pl.ds(half * HALF, HALF)]
+        remote(part, part, ROOT, one_r.at[3 + half], sibling).start()
+    received(one_r.at[4], grad.at[pl.ds(0, HALF), :])
+    left = product(split(roots[0, pl.ds(c * HALF, HALF), :]), gsplit)
+    received(one_r.at[3], grad.at[pl.ds(0, HALF), :])
     result = product(split(left), split(roots[1]))
     for i in range(PIECES):
         precond[i] = result[i * ROWS : (i + 1) * ROWS]
@@ -340,13 +344,8 @@
     def place(xt, zt):
         return (xt * 2 + zt) * 2 + c
 
-    gathers = []
-
-    def spread(i, d2d, source, xt, zt):
-        where = gath.at[place(xt, zt), rows_of(i)]
-        copy = remote(source, where, gd_s.at[d2d], gd_r.at[d2d], sibling)
-        copy.start()
-        gathers.append(copy)
+    def spread(i, source, xt, zt):
+        remote(source, gath.at[place(xt, zt), rows_of(i)], SPREAD, one_r.at[5], sibling).start()
 
     def gather_copy(phase, d, step, q):
         index = ((phase * 2 + d) * 3 + step) * QS + q
@@ -354,12 +353,10 @@
         zt = zh if phase == 0 else 1 - zh
         where = gath.at[place(xt, zt), rows_of(d * QS + q)]
         source = precond.at[d * QS + q] if phase == 0 and step == 0 else where
-        return remote(source, where, gr_s.at[index], gr_r.at[index], side[d])
+        return remote(source, where, GRING, ring_r.at[index], side[d])
 
     def gather_start(phase, d, step, q):
-        copy = gather_copy(phase, d, step, q)
-        copy.start()
-        gathers.append(copy)
+        gather_copy(phase, d, step, q).start()
 
     def gather_take(phase, d, step, q):
         gather_copy(phase, d, step, q).wait_recv()
@@ -367,60 +364,78 @@
             gather_start(phase, d, step + 1, q)
         xt = (x + 3 - step) % 4 if d == 0 else (x + 1 + step) % 4
         zt = zh if phase == 0 else 1 - zh
-        spread(d * QS + q, (phase * 4 + step + 1) * PIECES + d * QS + q, gath.at[place(xt, zt), rows_of(d * QS + q)], xt, zt)
+        spread(d * QS + q, gath.at[place(xt, zt), rows_of(d * QS + q)], xt, zt)
 
     mates = [
-        remote(precond.at[i], gath.at[place(x, zh), rows_of(i)], gz_s.at[i], gz_r.at[i], zmate)
-        for i in range(PIECES)
+        remote(precond.at[i], gath.at[place(x, zh), rows_of(i)], GZ, z_r.at[i], zmate) for i in range(PIECES)
     ]
     order = [(d, q) for q in range(QS) for d in range(2)]
     for d, q in order:
         mates[d * QS + q].start()
         gather_start(0, d, 0, q)
     for i in range(PIECES):
-        spread(i, i, precond.at[i], x, zh)
+        spread(i, precond.at[i], x, zh)
         gath[place(x, zh), rows_of(i)] = precond[i]
 
     def mate_take(d, q):
         i = d * QS + q
         mates[i].wait_recv()
         gather_start(1, d, 0, q)
-        spread(i, 4 * PIECES + i, gath.at[place(x, 1 - zh), rows_of(i)], x, 1 - zh)
-
-    for d, q in order:
-        gather_take(0, d, 0, q)
+        spread(i, gath.at[place(x, 1 - zh), rows_of(i)], x, 1 - zh)
+
+    def takes(phase, step, qs):
+        for q in qs:
+            for d in range(2):
+                gather_take(phase, d, step, q)
+
+    def mate_takes(q):
+        for d in range(2):
+            mate_take(d, q)
+
+    takes(0, 0, range(4))
     value = stage_take(1, 0)
     stage_start(1, 1, value)
-    mate_take(0, 0)
-    for d, q in order:
-        gather_take(0, d, 1, q)
+    mate_takes(0)
+    takes(0, 1, range(4))
     value = stage_take(1, 1)
     stage_start(1, 2, value)
-    mate_take(1, 0)
-    for d, q in order:
-        gather_take(0, d, 2, q)
-    for q in range(1, QS):
-        for d in range(2):
-            mate_take(d, q)
+    mate_takes(1)
 
     @pl.when(moves)
     def _():
-        for copy in back_remote:
-            copy.wait()
+        received(one_r.at[1], triangle)
         mirror(new_stat)
 
-    for step in range(3):
-        for d, q in order:
-            gather_take(1, d, step, q)
+    takes(1, 0, (0,))
+    mate_takes(2)
+    takes(1, 0, (1,))
+    takes(1, 1, (0,))
+    takes(0, 2, range(4))
+    mate_takes(3)
+    takes(1, 0, (2,))
+    takes(1, 1, (1,))
+    takes(1, 2, (0,))
+    takes(1, 0, (3,))
+    takes(1, 1, (2,))
+    takes(1, 2, (1,))
+    takes(1, 1, (3,))
+    takes(1, 2, (2, 3))
     value = stage_take(1, 2)
     prec_sq = total(jnp.where(top & (lane == 0), value, 0.0))
     scale_out[...] = jnp.broadcast_to(jnp.sqrt(grad_sq / (prec_sq + EPS)), (8, 128))
 
-    for i in range(8 * PIECES):
-        where = gath.at[0, rows_of(i % PIECES)]
-        remote(where, where, gd_s.at[i], gd_r.at[i], sibling).wait_recv()
-    for copy in pair + started + zcopies + gcopies + sum_copies + [root_copy] + gathers + mates:
-        copy.wait_send()
+    received(one_r.at[5], acc)
+    for kind, size in (
+        (PAIR, psend), (RING, psend.at[pl.ds(0, 6)]), (ZX, psend.at[0]), (GRAD, psend.at[0]),
+        (SUMS, sums.at[pl.ds(0, 34)]), (ROOT, psend.at[pl.ds(0, 2)]), (GRING, psend.at[pl.ds(0, 6)]),
+        (GZ, psend.at[0]), (SPREAD, psend),
+    ):
+        sent(kind, size)
+
+    @pl.when(moves)
+    def _():
+        sent(ST, triangle)
+        sent(NS, triangle)
 
 
 def run_main(blocks, act, og, stat):
@@ -454,10 +469,7 @@
             pltpu.VMEM((2, BLOCK, BLOCK), f32),
             pltpu.VMEM((PIECES, ROWS, BLOCK), f32),
             pltpu.VMEM((40, 8, 128), f32),
-            dma((8,)), dma((8,)), dma((ring_count,)), dma((ring_count,)), dma((PIECES,)), dma((PIECES,)),
-            dma((PIECES,)), dma((PIECES,)), dma((4,)), dma((4,)), dma((4,)), dma((4,)), dma(()), dma(()),
-            dma((ring_count,)), dma((ring_count,)), dma((PIECES,)), dma((PIECES,)),
-            dma((8 * PIECES,)), dma((8 * PIECES,)), dma(()), dma((40,)), dma((40,)), dma((6,)),
+            dma((11,)), dma((8,)), dma((ring_count,)), dma((PIECES,)), dma((6,)), dma((6,)), dma(()), dma((6,)),
         ],
         compiler_params=pltpu.CompilerParams(
             collective_id=0, has_side_effects=True, vmem_limit_bytes=40 * 1024 * 1024

time: 128 us -> 120 us (0.938)
  the two profiles are of different devices: /device:TPU:33 before, /device:TPU:1 now
where the time goes in v4:
time: 120 us
  Pallas kernels  119 us (99%)
    pallas_call x1, Pallas kernels, run_main(): pl.pallas_call(main_kernel, out_shape=(jax.ShapeDtypeStruct((16, HALF, BL...  114 us
    pallas_call x1, Pallas kernels, run_place(): pl.pallas_call(place_kernel, in_specs=[pl.BlockSpec(memory_space=pltpu.SM...  4.4 us

profile of v4, /device:TPU:1, one launch (start us, length us, event | category | flops | bytes accessed | tf_op | source)
XLA Modules:
  0.0 119.5 jit_solution(15576776138570192216)
XLA Ops:
  0.6 114.5 %shampoo.1 = (f32[16,256,512]{2,1,0:T(8,128)S(1)}, f32[512,512]{1,0:T(8,128)S(1)}, f32[8,128]{1,0:T(8,128)S(1)}) custom-call(s32[1,8]{1,0:T(1,128)} %blocks.3, bf16[256,4096]{1,0:T(8,128)(2,1)} %act_in.1, bf16[256,512]{1,0:T(8,128)(2,1)} %og_in.1, f32[512,512]{1,0:T(8,128)} %bitcast.2), custom_call_target="tpu_custom_call" | custom-call | tf_op jit(solution)/shard_map/shampoo/pallas_call | solution.py:445
  115.1 4.4 %place.1 = (f32[4096,512]{1,0:T(8,128)}, f32[512,512]{1,0:T(8,128)}) custom-call(s32[1,8]{1,0:T(1,128)} %blocks.3, f32[16,256,512]{2,1,0:T(8,128)S(1)} %get-tuple-element.7.gath, f32[512,512]{1,0:T(8,128)S(1)} %get-tuple-element.8.stat_in, f32[8,128]{1,0:T(8,128)S(1)} %get-tuple-element.9.scale), custom_call_target="tpu_custom_call" | custom-call | tf_op jit(solution)/shard_map/place/pallas_call | solution.py:503

commit v5 on v4

--- a/solution.py
+++ b/solution.py
@@ -19,8 +19,8 @@
 EPS = 1e-06
 COUNT = 131072.0
 
-RELATIVE = (3, 1, 2, 0)
-SEQUENCE = ((0, 2, 1, 3), (1, 2, 0, 3))
+RELATIVE = (2, 3, 1, 0)
+SOURCES = ((0, 2, 1), (0, 1, 2))
 QS = 4
 ROWS = HALF // 2 // QS
 PIECES = 2 * QS
@@ -141,18 +141,22 @@
             columns(slot, half), og[...], (((0,), (0,)), ((), ())), preferred_element_type=f32
         )
 
-    def ring_copy(phase, d, step, q):
-        index = ((phase * 2 + d) * 3 + step) * QS + q
-        source = acc.at[phase * 4 + SEQUENCE[d][step], rows_of(d * QS + q)]
-        return remote(source, ring.at[index], RING, ring_r.at[index], side[d])
-
-    def ring_start(phase, d, step, q):
-        ring_copy(phase, d, step, q).start()
-
-    def ring_take(phase, d, step, q):
-        index = ((phase * 2 + d) * 3 + step) * QS + q
-        ring_copy(phase, d, step, q).wait_recv()
-        slot = phase * 4 + SEQUENCE[d][step + 1]
+    def to_side(d, kind):
+        return side[1 - d if kind == 2 else d]
+
+    def ring_copy(phase, d, kind, q):
+        index = ((phase * 2 + d) * 3 + kind) * QS + q
+        source = acc.at[phase * 4 + SOURCES[d][kind], rows_of(d * QS + q)]
+        return remote(source, ring.at[index], RING, ring_r.at[index], to_side(d, kind))
+
+    def ring_start(phase, kind, q):
+        for d in range(2):
+            ring_copy(phase, d, kind, q).start()
+
+    def ring_take(phase, d, kind, q):
+        index = ((phase * 2 + d) * 3 + kind) * QS + q
+        ring_copy(phase, d, kind, q).wait_recv()
+        slot = phase * 4 + (SOURCES[d][1] if kind == 0 else 3)
         rows = rows_of(d * QS + q)
         acc[slot, rows] = acc[slot, rows] + ring[index]
 
@@ -174,45 +178,43 @@
         pair_start(slot)
         acc[slot] = partial(slot, c)
 
-    def advance(phase, step, qs):
+    def advance(phase, qs):
         for q in qs:
+            ring_start(phase, 2, q)
             for d in range(2):
-                ring_take(phase, d, step, q)
-                ring_start(phase, d, step + 1, q)
+                ring_take(phase, d, 0, q)
+            ring_start(phase, 1, q)
 
     zcopies = [remote(acc.at[3, rows_of(i)], zbuf.at[i], ZX, z_r.at[i], zmate) for i in range(PIECES)]
     pair_start(0)
     pair_start(1)
-    for slot in range(2):
+    pair_start(2)
+    acc[0] = partial(0, c)
+    pair_take(0)
+    for q in range(QS):
+        ring_start(0, 0, q)
+    for slot in range(1, 3):
         acc[slot] = partial(slot, c)
         pair_take(slot)
-        for q in range(QS):
-            ring_start(0, slot, 0, q)
-    make(2)
+    advance(0, (0, 1))
     make(3)
-    pair_take(2)
-    advance(0, 0, (0, 1))
     make(4)
     pair_take(3)
-    advance(0, 0, (2, 3))
-    make(5)
+    advance(0, (2, 3))
     pair_take(4)
-    advance(0, 1, (0, 1))
-    make(6)
-    pair_take(5)
-    advance(0, 1, (2, 3))
+    for q in range(QS):
+        ring_start(1, 0, q)
+    for slot in range(5, 8):
+        make(slot)
+        if slot > 5:
+            pair_take(slot - 1)
+    pair_take(7)
     for q in range(QS):
         for d in range(2):
-            ring_start(1, d, 0, q)
-    make(7)
-    pair_take(6)
-    for q in range(QS):
-        for d in range(2):
-            ring_take(0, d, 2, q)
+            for kind in (2, 1):
+                ring_take(0, d, kind, q)
             zcopies[d * QS + q].start()
-    pair_take(7)
-    advance(1, 0, range(4))
-    advance(1, 1, range(4))
+    advance(1, range(4))
 
     @pl.when(moves)
     def _():
@@ -222,7 +224,8 @@
     for q in range(QS):
         for d in range(2):
             i = d * QS + q
-            ring_take(1, d, 2, q)
+            for kind in (2, 1):
+                ring_take(1, d, kind, q)
             zcopies[i].wait_recv()
             here = pl.ds(c * HALF + i * ROWS, ROWS)
             grad[here, :] = acc[7, rows_of(i)] + zbuf[i]
@@ -265,6 +268,8 @@
 
     value = stage_take(0, 0)
     stage_start(0, 1, value)
+    value = stage_take(0, 1)
+    stage_start(0, 2, value)
 
     @pl.when(stays)
     def _():
@@ -277,8 +282,16 @@
 
     now = DECAY * stat[...] + norm[0]
     stat[...] = now
-    value = stage_take(0, 1)
-    stage_start(0, 2, value)
+
+    @pl.when(stays)
+    def _():
+        new_stat[...] = now
+
+    @pl.when(moves)
+    def _():
+        for copy in back_remote:
+            copy.start()
+
     square_sum = total(now * now)
     now_trace = total(jnp.where(mask, now, 0.0))
     size = jnp.sqrt(square_sum + EPS)
@@ -291,16 +304,6 @@
     norm[2] = third
 
     value = stage_take(0, 2)
-
-    @pl.when(stays)
-    def _():
-        new_stat[...] = stat[...]
-
-    @pl.when(moves)
-    def _():
-        for copy in back_remote:
-            copy.start()
-
     top = lax.broadcasted_iota(jnp.int32, (8, 128), 0) == 0
     trace_all = total(jnp.where(top & (lane == 0), value, 0.0))
     grad_sq = total(jnp.where(top & (lane == 1), value, 0.0))
@@ -347,56 +350,53 @@
     def spread(i, source, xt, zt):
         remote(source, gath.at[place(xt, zt), rows_of(i)], SPREAD, one_r.at[5], sibling).start()
 
-    def gather_copy(phase, d, step, q):
-        index = ((phase * 2 + d) * 3 + step) * QS + q
-        xt = (x + 4 - step) % 4 if d == 0 else (x + step) % 4
+    def gather_copy(phase, d, kind, q):
+        index = ((phase * 2 + d) * 3 + kind) * QS + q
+        xt = x if kind != 1 else (x + 3 + 2 * d) % 4
         zt = zh if phase == 0 else 1 - zh
         where = gath.at[place(xt, zt), rows_of(d * QS + q)]
-        source = precond.at[d * QS + q] if phase == 0 and step == 0 else where
-        return remote(source, where, GRING, ring_r.at[index], side[d])
-
-    def gather_start(phase, d, step, q):
-        gather_copy(phase, d, step, q).start()
-
-    def gather_take(phase, d, step, q):
-        gather_copy(phase, d, step, q).wait_recv()
-        if step < 2:
-            gather_start(phase, d, step + 1, q)
-        xt = (x + 3 - step) % 4 if d == 0 else (x + 1 + step) % 4
+        source = precond.at[d * QS + q] if phase == 0 and kind != 1 else where
+        return remote(source, where, GRING, ring_r.at[index], to_side(d, kind))
+
+    def gather_take(phase, d, kind, q):
+        gather_copy(phase, d, kind, q).wait_recv()
+        if kind == 0:
+            gather_copy(phase, d, 1, q).start()
+        xt = (x + (3 + 2 * d, 2, 1 + 2 * d)[kind]) % 4
         zt = zh if phase == 0 else 1 - zh
         spread(d * QS + q, gath.at[place(xt, zt), rows_of(d * QS + q)], xt, zt)
 
     mates = [
         remote(precond.at[i], gath.at[place(x, zh), rows_of(i)], GZ, z_r.at[i], zmate) for i in range(PIECES)
     ]
-    order = [(d, q) for q in range(QS) for d in range(2)]
-    for d, q in order:
-        mates[d * QS + q].start()
-        gather_start(0, d, 0, q)
+    for kind in (0, 2):
+        for q in range(QS):
+            for d in range(2):
+                if kind == 0:
+                    mates[d * QS + q].start()
+                gather_copy(0, d, kind, q).start()
     for i in range(PIECES):
         spread(i, precond.at[i], x, zh)
         gath[place(x, zh), rows_of(i)] = precond[i]
 
-    def mate_take(d, q):
-        i = d * QS + q
-        mates[i].wait_recv()
-        gather_start(1, d, 0, q)
-        spread(i, gath.at[place(x, 1 - zh), rows_of(i)], x, 1 - zh)
-
-    def takes(phase, step, qs):
+    def mate_takes(q):
+        for d in range(2):
+            i = d * QS + q
+            mates[i].wait_recv()
+            gather_copy(1, d, 0, q).start()
+            gather_copy(1, d, 2, q).start()
+            spread(i, gath.at[place(x, 1 - zh), rows_of(i)], x, 1 - zh)
+
+    def takes(phase, kind, qs):
         for q in qs:
             for d in range(2):
-                gather_take(phase, d, step, q)
-
-    def mate_takes(q):
-        for d in range(2):
-            mate_take(d, q)
+                gather_take(phase, d, kind, q)
 
     takes(0, 0, range(4))
     value = stage_take(1, 0)
     stage_start(1, 1, value)
     mate_takes(0)
-    takes(0, 1, range(4))
+    takes(0, 2, range(4))
     value = stage_take(1, 1)
     stage_start(1, 2, value)
     mate_takes(1)
@@ -406,20 +406,17 @@
         received(one_r.at[1], triangle)
         mirror(new_stat)
 
-    takes(1, 0, (0,))
+    takes(0, 1, range(4))
     mate_takes(2)
-    takes(1, 0, (1,))
-    takes(1, 1, (0,))
-    takes(0, 2, range(4))
+    takes(1, 0, (0, 1))
+    takes(1, 2, (0, 1))
     mate_takes(3)
     takes(1, 0, (2,))
-    takes(1, 1, (1,))
-    takes(1, 2, (0,))
+    takes(1, 2, (2,))
+    takes(1, 1, (0, 1))
     takes(1, 0, (3,))
-    takes(1, 1, (2,))
-    takes(1, 2, (1,))
-    takes(1, 1, (3,))
-    takes(1, 2, (2, 3))
+    takes(1, 2, (3,))
+    takes(1, 1, (2, 3))
     value = stage_take(1, 2)
     prec_sq = total(jnp.where(top & (lane == 0), value, 0.0))
     scale_out[...] = jnp.broadcast_to(jnp.sqrt(grad_sq / (prec_sq + EPS)), (8, 128))

time: 120 us -> 120 us (level)
  no operation moved by 1% of the time
where the time goes in v5:
time: 120 us; the launch traced here: 119 us
  Pallas kernels  119 us (99%)
    pallas_call x1, Pallas kernels, run_main(): pl.pallas_call(main_kernel, out_shape=(jax.ShapeDtypeStruct((16, HALF, BL...  114 us
    pallas_call x1, Pallas kernels, run_place(): pl.pallas_call(place_kernel, in_specs=[pl.BlockSpec(memory_space=pltpu.SM...  4.4 us

profile of v5, /device:TPU:1, one launch (start us, length us, event | category | flops | bytes accessed | tf_op | source)
XLA Modules:
  0.0 119.2 jit_solution(12306745403639568038)
XLA Ops:
  0.6 114.1 %shampoo.1 = (f32[16,256,512]{2,1,0:T(8,128)S(1)}, f32[512,512]{1,0:T(8,128)S(1)}, f32[8,128]{1,0:T(8,128)S(1)}) custom-call(s32[1,8]{1,0:T(1,128)} %blocks.3, bf16[256,4096]{1,0:T(8,128)(2,1)} %act_in.1, bf16[256,512]{1,0:T(8,128)(2,1)} %og_in.1, f32[512,512]{1,0:T(8,128)} %bitcast.2), custom_call_target="tpu_custom_call" | custom-call | tf_op jit(solution)/shard_map/shampoo/pallas_call | solution.py:442
  114.8 4.4 %place.1 = (f32[4096,512]{1,0:T(8,128)}, f32[512,512]{1,0:T(8,128)}) custom-call(s32[1,8]{1,0:T(1,128)} %blocks.3, f32[16,256,512]{2,1,0:T(8,128)S(1)} %get-tuple-element.7.gath, f32[512,512]{1,0:T(8,128)S(1)} %get-tuple-element.8.stat_in, f32[8,128]{1,0:T(8,128)S(1)} %get-tuple-element.9.scale), custom_call_target="tpu_custom_call" | custom-call | tf_op jit(solution)/shard_map/place/pallas_call | solution.py:500

commit v6 on v5

--- a/solution.py
+++ b/solution.py
@@ -350,53 +350,56 @@
     def spread(i, source, xt, zt):
         remote(source, gath.at[place(xt, zt), rows_of(i)], SPREAD, one_r.at[5], sibling).start()
 
-    def gather_copy(phase, d, kind, q):
-        index = ((phase * 2 + d) * 3 + kind) * QS + q
-        xt = x if kind != 1 else (x + 3 + 2 * d) % 4
+    def gather_copy(phase, d, step, q):
+        index = ((phase * 2 + d) * 3 + step) * QS + q
+        xt = (x + 4 - step) % 4 if d == 0 else (x + step) % 4
         zt = zh if phase == 0 else 1 - zh
         where = gath.at[place(xt, zt), rows_of(d * QS + q)]
-        source = precond.at[d * QS + q] if phase == 0 and kind != 1 else where
-        return remote(source, where, GRING, ring_r.at[index], to_side(d, kind))
-
-    def gather_take(phase, d, kind, q):
-        gather_copy(phase, d, kind, q).wait_recv()
-        if kind == 0:
-            gather_copy(phase, d, 1, q).start()
-        xt = (x + (3 + 2 * d, 2, 1 + 2 * d)[kind]) % 4
+        source = precond.at[d * QS + q] if phase == 0 and step == 0 else where
+        return remote(source, where, GRING, ring_r.at[index], side[d])
+
+    def gather_start(phase, d, step, q):
+        gather_copy(phase, d, step, q).start()
+
+    def gather_take(phase, d, step, q):
+        gather_copy(phase, d, step, q).wait_recv()
+        if step < 2:
+            gather_start(phase, d, step + 1, q)
+        xt = (x + 3 - step) % 4 if d == 0 else (x + 1 + step) % 4
         zt = zh if phase == 0 else 1 - zh
         spread(d * QS + q, gath.at[place(xt, zt), rows_of(d * QS + q)], xt, zt)
 
     mates = [
         remote(precond.at[i], gath.at[place(x, zh), rows_of(i)], GZ, z_r.at[i], zmate) for i in range(PIECES)
     ]
-    for kind in (0, 2):
-        for q in range(QS):
-            for d in range(2):
-                if kind == 0:
-                    mates[d * QS + q].start()
-                gather_copy(0, d, kind, q).start()
+    order = [(d, q) for q in range(QS) for d in range(2)]
+    for d, q in order:
+        mates[d * QS + q].start()
+        gather_start(0, d, 0, q)
     for i in range(PIECES):
         spread(i, precond.at[i], x, zh)
         gath[place(x, zh), rows_of(i)] = precond[i]
 
+    def mate_take(d, q):
+        i = d * QS + q
+        mates[i].wait_recv()
+        gather_start(1, d, 0, q)
+        spread(i, gath.at[place(x, 1 - zh), rows_of(i)], x, 1 - zh)
+
+    def takes(phase, step, qs):
+        for q in qs:
+            for d in range(2):
+                gather_take(phase, d, step, q)
+
     def mate_takes(q):
         for d in range(2):
-            i = d * QS + q
-            mates[i].wait_recv()
-            gather_copy(1, d, 0, q).start()
-            gather_copy(1, d, 2, q).start()
-            spread(i, gath.at[place(x, 1 - zh), rows_of(i)], x, 1 - zh)
-
-    def takes(phase, kind, qs):
-        for q in qs:
-            for d in range(2):
-                gather_take(phase, d, kind, q)
+            mate_take(d, q)
 
     takes(0, 0, range(4))
     value = stage_take(1, 0)
     stage_start(1, 1, value)
     mate_takes(0)
-    takes(0, 2, range(4))
+    takes(0, 1, range(4))
     value = stage_take(1, 1)
     stage_start(1, 2, value)
     mate_takes(1)
@@ -406,17 +409,20 @@
         received(one_r.at[1], triangle)
         mirror(new_stat)
 
-    takes(0, 1, range(4))
+    takes(1, 0, (0,))
     mate_takes(2)
-    takes(1, 0, (0, 1))
-    takes(1, 2, (0, 1))
+    takes(1, 0, (1,))
+    takes(1, 1, (0,))
+    takes(0, 2, range(4))
     mate_takes(3)
     takes(1, 0, (2,))
-    takes(1, 2, (2,))
-    takes(1, 1, (0, 1))
+    takes(1, 1, (1,))
+    takes(1, 2, (0,))
     takes(1, 0, (3,))
-    takes(1, 2, (3,))
-    takes(1, 1, (2, 3))
+    takes(1, 1, (2,))
+    takes(1, 2, (1,))
+    takes(1, 1, (3,))
+    takes(1, 2, (2, 3))
     value = stage_take(1, 2)
     prec_sq = total(jnp.where(top & (lane == 0), value, 0.0))
     scale_out[...] = jnp.broadcast_to(jnp.sqrt(grad_sq / (prec_sq + EPS)), (8, 128))

time: 120 us -> 127 us (1.058)
  Pallas kernels: 119 us -> 126 us
    pallas_call x1, Pallas kernels: 114 us -> 122 us  [run_main(): pl.pallas_call(main_kernel, out_shape=(jax.ShapeDtypeStruct((16, HALF, BL...]
where the time goes in v6:
time: 127 us
  Pallas kernels  126 us (99%)
    pallas_call x1, Pallas kernels, run_main(): pl.pallas_call(main_kernel, out_shape=(jax.ShapeDtypeStruct((16, HALF, BL...  122 us
    pallas_call x1, Pallas kernels, run_place(): pl.pallas_call(place_kernel, in_specs=[pl.BlockSpec(memory_space=pltpu.SM...  4.4 us

profile of v6, /device:TPU:1, one launch (start us, length us, event | category | flops | bytes accessed | tf_op | source)
XLA Modules:
  0.0 126.8 jit_solution(11661160507636035290)
XLA Ops:
  0.6 121.7 %shampoo.1 = (f32[16,256,512]{2,1,0:T(8,128)S(1)}, f32[512,512]{1,0:T(8,128)S(1)}, f32[8,128]{1,0:T(8,128)S(1)}) custom-call(s32[1,8]{1,0:T(1,128)} %blocks.3, bf16[256,4096]{1,0:T(8,128)(2,1)} %act_in.1, bf16[256,512]{1,0:T(8,128)(2,1)} %og_in.1, f32[512,512]{1,0:T(8,128)} %bitcast.2), custom_call_target="tpu_custom_call" | custom-call | tf_op jit(solution)/shard_map/shampoo/pallas_call | solution.py:448
  122.4 4.4 %place.1 = (f32[4096,512]{1,0:T(8,128)}, f32[512,512]{1,0:T(8,128)}) custom-call(s32[1,8]{1,0:T(1,128)} %blocks.3, f32[16,256,512]{2,1,0:T(8,128)S(1)} %get-tuple-element.7.gath, f32[512,512]{1,0:T(8,128)S(1)} %get-tuple-element.8.stat_in, f32[8,128]{1,0:T(8,128)S(1)} %get-tuple-element.9.scale), custom_call_target="tpu_custom_call" | custom-call | tf_op jit(solution)/shard_map/place/pallas_call | solution.py:506

commit v7 on v5

--- a/solution.py
+++ b/solution.py
@@ -283,15 +283,6 @@
     now = DECAY * stat[...] + norm[0]
     stat[...] = now
 
-    @pl.when(stays)
-    def _():
-        new_stat[...] = now
-
-    @pl.when(moves)
-    def _():
-        for copy in back_remote:
-            copy.start()
-
     square_sum = total(now * now)
     now_trace = total(jnp.where(mask, now, 0.0))
     size = jnp.sqrt(square_sum + EPS)
@@ -304,6 +295,16 @@
     norm[2] = third
 
     value = stage_take(0, 2)
+
+    @pl.when(stays)
+    def _():
+        new_stat[...] = stat[...]
+
+    @pl.when(moves)
+    def _():
+        for copy in back_remote:
+            copy.start()
+
     top = lax.broadcasted_iota(jnp.int32, (8, 128), 0) == 0
     trace_all = total(jnp.where(top & (lane == 0), value, 0.0))
     grad_sq = total(jnp.where(top & (lane == 1), value, 0.0))

time: 120 us -> 116 us (0.967)
  Pallas kernels: 119 us -> 115 us
    pallas_call x1, Pallas kernels: 114 us -> 110 us  [run_main(): pl.pallas_call(main_kernel, out_shape=(jax.ShapeDtypeStruct((16, HALF, BL...]
where the time goes in v7:
time: 116 us
  Pallas kernels  115 us (99%)
    pallas_call x1, Pallas kernels, run_main(): pl.pallas_call(main_kernel, out_shape=(jax.ShapeDtypeStruct((16, HALF, BL...  110 us
    pallas_call x1, Pallas kernels, run_place(): pl.pallas_call(place_kernel, in_specs=[pl.BlockSpec(memory_space=pltpu.SM...  4.4 us

profile of v7, /device:TPU:1, one launch (start us, length us, event | category | flops | bytes accessed | tf_op | source)
XLA Modules:
  0.0 115.5 jit_solution(2303526352953970641)
XLA Ops:
  0.6 110.5 %shampoo.1 = (f32[16,256,512]{2,1,0:T(8,128)S(1)}, f32[512,512]{1,0:T(8,128)S(1)}, f32[8,128]{1,0:T(8,128)S(1)}) custom-call(s32[1,8]{1,0:T(1,128)} %blocks.3, bf16[256,4096]{1,0:T(8,128)(2,1)} %act_in.1, bf16[256,512]{1,0:T(8,128)(2,1)} %og_in.1, f32[512,512]{1,0:T(8,128)} %bitcast.2), custom_call_target="tpu_custom_call" | custom-call | tf_op jit(solution)/shard_map/shampoo/pallas_call | solution.py:443
  111.1 4.4 %place.1 = (f32[4096,512]{1,0:T(8,128)}, f32[512,512]{1,0:T(8,128)}) custom-call(s32[1,8]{1,0:T(1,128)} %blocks.3, f32[16,256,512]{2,1,0:T(8,128)S(1)} %get-tuple-element.7.gath, f32[512,512]{1,0:T(8,128)S(1)} %get-tuple-element.8.stat_in, f32[8,128]{1,0:T(8,128)S(1)} %get-tuple-element.9.scale), custom_call_target="tpu_custom_call" | custom-call | tf_op jit(solution)/shard_map/place/pallas_call | solution.py:501

commit v8 on v7

--- a/solution.py
+++ b/solution.py
@@ -24,6 +24,7 @@
 QS = 4
 ROWS = HALF // 2 // QS
 PIECES = 2 * QS
+LAST = PIECES - 1
 PAIR, RING, ZX, GRAD, ST, NS, SUMS, ROOT, GRING, GZ, SPREAD = range(11)
 
 
@@ -149,8 +150,11 @@
         source = acc.at[phase * 4 + SOURCES[d][kind], rows_of(d * QS + q)]
         return remote(source, ring.at[index], RING, ring_r.at[index], to_side(d, kind))
 
+    def halves(phase, q):
+        return [d for d in range(2) if phase == 1 or d * QS + q != LAST]
+
     def ring_start(phase, kind, q):
-        for d in range(2):
+        for d in halves(phase, q):
             ring_copy(phase, d, kind, q).start()
 
     def ring_take(phase, d, kind, q):
@@ -181,11 +185,19 @@
     def advance(phase, qs):
         for q in qs:
             ring_start(phase, 2, q)
-            for d in range(2):
+            for d in halves(phase, q):
                 ring_take(phase, d, 0, q)
             ring_start(phase, 1, q)
 
-    zcopies = [remote(acc.at[3, rows_of(i)], zbuf.at[i], ZX, z_r.at[i], zmate) for i in range(PIECES)]
+    zcopies = [remote(acc.at[3, rows_of(i)], zbuf.at[i], ZX, z_r.at[i], zmate) for i in range(LAST)]
+    zfirst = [
+        remote(acc.at[k, rows_of(LAST)], zbuf.at[LAST + k], ZX, z_r.at[LAST + k], zmate) for k in range(4)
+    ]
+
+    def zfirst_take(k):
+        zfirst[k].wait_recv()
+        acc[4 + k, rows_of(LAST)] = acc[4 + k, rows_of(LAST)] + zbuf[LAST + k]
+
     pair_start(0)
     pair_start(1)
     pair_start(2)
@@ -193,27 +205,34 @@
     pair_take(0)
     for q in range(QS):
         ring_start(0, 0, q)
+    zfirst[0].start()
     for slot in range(1, 3):
         acc[slot] = partial(slot, c)
         pair_take(slot)
+        zfirst[slot].start()
     advance(0, (0, 1))
     make(3)
     make(4)
     pair_take(3)
+    zfirst[3].start()
     advance(0, (2, 3))
     pair_take(4)
-    for q in range(QS):
+    for q in range(QS - 1):
         ring_start(1, 0, q)
+    zfirst_take(0)
+    ring_start(1, 0, QS - 1)
     for slot in range(5, 8):
         make(slot)
         if slot > 5:
             pair_take(slot - 1)
     pair_take(7)
     for q in range(QS):
-        for d in range(2):
+        for d in halves(0, q):
             for kind in (2, 1):
                 ring_take(0, d, kind, q)
             zcopies[d * QS + q].start()
+    for k in range(1, 4):
+        zfirst_take(k)
     advance(1, range(4))
 
     @pl.when(moves)
@@ -226,9 +245,12 @@
             i = d * QS + q
             for kind in (2, 1):
                 ring_take(1, d, kind, q)
-            zcopies[i].wait_recv()
             here = pl.ds(c * HALF + i * ROWS, ROWS)
-            grad[here, :] = acc[7, rows_of(i)] + zbuf[i]
+            if i == LAST:
+                grad[here, :] = acc[7, rows_of(i)]
+            else:
+                zcopies[i].wait_recv()
+                grad[here, :] = acc[7, rows_of(i)] + zbuf[i]
             remote(grad.at[here, :], grad.at[here, :], GRAD, one_r.at[2], sibling).start()
 
     lane = lax.broadcasted_iota(jnp.int32, (8, 128), 1)
@@ -365,23 +387,35 @@
             gather_copy(phase, d, 1, q).start()
         xt = (x + (3 + 2 * d, 2, 1 + 2 * d)[kind]) % 4
         zt = zh if phase == 0 else 1 - zh
+        if phase == 0 and d * QS + q == LAST:
+            last_copy(xt, zt, (kind + 1)).start()
         spread(d * QS + q, gath.at[place(xt, zt), rows_of(d * QS + q)], xt, zt)
 
+    def last_copy(xt, zt, k):
+        where = gath.at[place(xt, zt), rows_of(LAST)]
+        source = precond.at[LAST] if k == 0 else where
+        return remote(source, where, GZ, z_r.at[LAST + k], zmate)
+
+    def last_take(k):
+        xt = x if k == 0 else (x + (5, 2, 3)[k - 1]) % 4
+        last_copy(xt, 1 - zh, k).wait_recv()
+        spread(LAST, gath.at[place(xt, 1 - zh), rows_of(LAST)], xt, 1 - zh)
+
     mates = [
-        remote(precond.at[i], gath.at[place(x, zh), rows_of(i)], GZ, z_r.at[i], zmate) for i in range(PIECES)
+        remote(precond.at[i], gath.at[place(x, zh), rows_of(i)], GZ, z_r.at[i], zmate) for i in range(LAST)
     ]
     for kind in (0, 2):
         for q in range(QS):
             for d in range(2):
                 if kind == 0:
-                    mates[d * QS + q].start()
+                    (last_copy(x, zh, 0) if d * QS + q == LAST else mates[d * QS + q]).start()
                 gather_copy(0, d, kind, q).start()
     for i in range(PIECES):
         spread(i, precond.at[i], x, zh)
         gath[place(x, zh), rows_of(i)] = precond[i]
 
     def mate_takes(q):
-        for d in range(2):
+        for d in halves(0, q):
             i = d * QS + q
             mates[i].wait_recv()
             gather_copy(1, d, 0, q).start()
@@ -390,7 +424,7 @@
 
     def takes(phase, kind, qs):
         for q in qs:
-            for d in range(2):
+            for d in halves(1 - phase, q):
                 gather_take(phase, d, kind, q)
 
     takes(0, 0, range(4))
@@ -417,16 +451,21 @@
     takes(1, 1, (0, 1))
     takes(1, 0, (3,))
     takes(1, 2, (3,))
-    takes(1, 1, (2, 3))
+    last_take(0)
+    last_take(1)
+    takes(1, 1, (2,))
+    last_take(3)
+    takes(1, 1, (3,))
+    last_take(2)
     value = stage_take(1, 2)
     prec_sq = total(jnp.where(top & (lane == 0), value, 0.0))
     scale_out[...] = jnp.broadcast_to(jnp.sqrt(grad_sq / (prec_sq + EPS)), (8, 128))
 
     received(one_r.at[5], acc)
     for kind, size in (
-        (PAIR, psend), (RING, psend.at[pl.ds(0, 6)]), (ZX, psend.at[0]), (GRAD, psend.at[0]),
-        (SUMS, sums.at[pl.ds(0, 34)]), (ROOT, psend.at[pl.ds(0, 2)]), (GRING, psend.at[pl.ds(0, 6)]),
-        (GZ, psend.at[0]), (SPREAD, psend),
+        (PAIR, psend), (RING, ring.at[pl.ds(0, 12 * QS - 3)]), (ZX, ring.at[pl.ds(0, LAST + 4)]), (GRAD, psend.at[0]),
+        (SUMS, sums.at[pl.ds(0, 34)]), (ROOT, psend.at[pl.ds(0, 2)]), (GRING, ring.at[pl.ds(0, 12 * QS - 3)]),
+        (GZ, ring.at[pl.ds(0, LAST + 4)]), (SPREAD, psend),
     ):
         sent(kind, size)
 
@@ -460,14 +499,14 @@
             pltpu.VMEM((8, HALF, BLOCK), f32),
             pltpu.VMEM((8, HALF, BLOCK), f32),
             pltpu.VMEM((ring_count, ROWS, BLOCK), f32),
-            pltpu.VMEM((PIECES, ROWS, BLOCK), f32),
+            pltpu.VMEM((LAST + 4, ROWS, BLOCK), f32),
             pltpu.VMEM((BLOCK, BLOCK), f32),
             pltpu.VMEM((BLOCK, BLOCK), f32),
             pltpu.VMEM((3, BLOCK, BLOCK), f32),
             pltpu.VMEM((2, BLOCK, BLOCK), f32),
             pltpu.VMEM((PIECES, ROWS, BLOCK), f32),
             pltpu.VMEM((40, 8, 128), f32),
-            dma((11,)), dma((8,)), dma((ring_count,)), dma((PIECES,)), dma((6,)), dma((6,)), dma(()), dma((6,)),
+            dma((11,)), dma((8,)), dma((ring_count,)), dma((LAST + 4,)), dma((6,)), dma((6,)), dma(()), dma((6,)),
         ],
         compiler_params=pltpu.CompilerParams(
             collective_id=0, has_side_effects=True, vmem_limit_bytes=40 * 1024 * 1024

time: 116 us -> 121 us (1.043)
  the two profiles are of different devices: /device:TPU:1 before, /device:TPU:99 now
where the time goes in v8:
time: 121 us
  Pallas kernels  121 us (100%)
    pallas_call x1, Pallas kernels, run_main(): pl.pallas_call(main_kernel, out_shape=(jax.ShapeDtypeStruct((16, HALF, BL...  116 us
    pallas_call x1, Pallas kernels, run_place(): pl.pallas_call(place_kernel, in_specs=[pl.BlockSpec(memory_space=pltpu.SM...  4.4 us

profile of v8, /device:TPU:99, one launch (start us, length us, event | category | flops | bytes accessed | tf_op | source)
XLA Modules:
  0.0 121.2 jit_solution(12683692215047217789)
XLA Ops:
  0.6 116.2 %shampoo.1 = (f32[16,256,512]{2,1,0:T(8,128)S(1)}, f32[512,512]{1,0:T(8,128)S(1)}, f32[8,128]{1,0:T(8,128)S(1)}) custom-call(s32[1,8]{1,0:T(1,128)} %blocks.3, bf16[256,4096]{1,0:T(8,128)(2,1)} %act_in.1, bf16[256,512]{1,0:T(8,128)(2,1)} %og_in.1, f32[512,512]{1,0:T(8,128)} %bitcast.2), custom_call_target="tpu_custom_call" | custom-call | tf_op jit(solution)/shard_map/shampoo/pallas_call | solution.py:482
  116.8 4.4 %place.1 = (f32[4096,512]{1,0:T(8,128)}, f32[512,512]{1,0:T(8,128)}) custom-call(s32[1,8]{1,0:T(1,128)} %blocks.3, f32[16,256,512]{2,1,0:T(8,128)S(1)} %get-tuple-element.7.gath, f32[512,512]{1,0:T(8,128)S(1)} %get-tuple-element.8.stat_in, f32[8,128]{1,0:T(8,128)S(1)} %get-tuple-element.9.scale), custom_call_target="tpu_custom_call" | custom-call | tf_op jit(solution)/shard_map/place/pallas_call | solution.py:540

commit v9 on v8

--- a/solution.py
+++ b/solution.py
@@ -387,35 +387,23 @@
             gather_copy(phase, d, 1, q).start()
         xt = (x + (3 + 2 * d, 2, 1 + 2 * d)[kind]) % 4
         zt = zh if phase == 0 else 1 - zh
-        if phase == 0 and d * QS + q == LAST:
-            last_copy(xt, zt, (kind + 1)).start()
         spread(d * QS + q, gath.at[place(xt, zt), rows_of(d * QS + q)], xt, zt)
 
-    def last_copy(xt, zt, k):
-        where = gath.at[place(xt, zt), rows_of(LAST)]
-        source = precond.at[LAST] if k == 0 else where
-        return remote(source, where, GZ, z_r.at[LAST + k], zmate)
-
-    def last_take(k):
-        xt = x if k == 0 else (x + (5, 2, 3)[k - 1]) % 4
-        last_copy(xt, 1 - zh, k).wait_recv()
-        spread(LAST, gath.at[place(xt, 1 - zh), rows_of(LAST)], xt, 1 - zh)
-
     mates = [
-        remote(precond.at[i], gath.at[place(x, zh), rows_of(i)], GZ, z_r.at[i], zmate) for i in range(LAST)
+        remote(precond.at[i], gath.at[place(x, zh), rows_of(i)], GZ, z_r.at[i], zmate) for i in range(PIECES)
     ]
     for kind in (0, 2):
         for q in range(QS):
             for d in range(2):
                 if kind == 0:
-                    (last_copy(x, zh, 0) if d * QS + q == LAST else mates[d * QS + q]).start()
+                    mates[d * QS + q].start()
                 gather_copy(0, d, kind, q).start()
     for i in range(PIECES):
         spread(i, precond.at[i], x, zh)
         gath[place(x, zh), rows_of(i)] = precond[i]
 
     def mate_takes(q):
-        for d in halves(0, q):
+        for d in range(2):
             i = d * QS + q
             mates[i].wait_recv()
             gather_copy(1, d, 0, q).start()
@@ -424,7 +412,7 @@
 
     def takes(phase, kind, qs):
         for q in qs:
-            for d in halves(1 - phase, q):
+            for d in range(2):
                 gather_take(phase, d, kind, q)
 
     takes(0, 0, range(4))
@@ -451,12 +439,7 @@
     takes(1, 1, (0, 1))
     takes(1, 0, (3,))
     takes(1, 2, (3,))
-    last_take(0)
-    last_take(1)
-    takes(1, 1, (2,))
-    last_take(3)
-    takes(1, 1, (3,))
-    last_take(2)
+    takes(1, 1, (2, 3))
     value = stage_take(1, 2)
     prec_sq = total(jnp.where(top & (lane == 0), value, 0.0))
     scale_out[...] = jnp.broadcast_to(jnp.sqrt(grad_sq / (prec_sq + EPS)), (8, 128))
@@ -464,8 +447,8 @@
     received(one_r.at[5], acc)
     for kind, size in (
         (PAIR, psend), (RING, ring.at[pl.ds(0, 12 * QS - 3)]), (ZX, ring.at[pl.ds(0, LAST + 4)]), (GRAD, psend.at[0]),
-        (SUMS, sums.at[pl.ds(0, 34)]), (ROOT, psend.at[pl.ds(0, 2)]), (GRING, ring.at[pl.ds(0, 12 * QS - 3)]),
-        (GZ, ring.at[pl.ds(0, LAST + 4)]), (SPREAD, psend),
+        (SUMS, sums.at[pl.ds(0, 34)]), (ROOT, psend.at[pl.ds(0, 2)]), (GRING, psend.at[pl.ds(0, 6)]),
+        (GZ, psend.at[0]), (SPREAD, psend),
     ):
         sent(kind, size)
 

time: 121 us -> 115 us (0.950)
  the two profiles are of different devices: /device:TPU:99 before, /device:TPU:1 now
where the time goes in v9:
time: 115 us; the launch traced here: 113 us
  Pallas kernels  112 us (97%)
    pallas_call x1, Pallas kernels, run_main(): pl.pallas_call(main_kernel, out_shape=(jax.ShapeDtypeStruct((16, HALF, BL...  108 us
    pallas_call x1, Pallas kernels, run_place(): pl.pallas_call(place_kernel, in_specs=[pl.BlockSpec(memory_space=pltpu.SM...  4.4 us

profile of v9, /device:TPU:1, one launch (start us, length us, event | category | flops | bytes accessed | tf_op | source)
XLA Modules:
  0.0 112.6 jit_solution(16021086642398242398)
XLA Ops:
  0.6 107.6 %shampoo.1 = (f32[16,256,512]{2,1,0:T(8,128)S(1)}, f32[512,512]{1,0:T(8,128)S(1)}, f32[8,128]{1,0:T(8,128)S(1)}) custom-call(s32[1,8]{1,0:T(1,128)} %blocks.3, bf16[256,4096]{1,0:T(8,128)(2,1)} %act_in.1, bf16[256,512]{1,0:T(8,128)(2,1)} %og_in.1, f32[512,512]{1,0:T(8,128)} %bitcast.2), custom_call_target="tpu_custom_call" | custom-call | tf_op jit(solution)/shard_map/shampoo/pallas_call | solution.py:465
  108.2 4.4 %place.1 = (f32[4096,512]{1,0:T(8,128)}, f32[512,512]{1,0:T(8,128)}) custom-call(s32[1,8]{1,0:T(1,128)} %blocks.3, f32[16,256,512]{2,1,0:T(8,128)S(1)} %get-tuple-element.7.gath, f32[512,512]{1,0:T(8,128)S(1)} %get-tuple-element.8.stat_in, f32[8,128]{1,0:T(8,128)S(1)} %get-tuple-element.9.scale), custom_call_target="tpu_custom_call" | custom-call | tf_op jit(solution)/shard_map/place/pallas_call | solution.py:523

commit v10 on v9

--- a/solution.py
+++ b/solution.py
@@ -424,11 +424,6 @@
     stage_start(1, 2, value)
     mate_takes(1)
 
-    @pl.when(moves)
-    def _():
-        received(one_r.at[1], triangle)
-        mirror(new_stat)
-
     takes(0, 1, range(4))
     mate_takes(2)
     takes(1, 0, (0, 1))
@@ -439,6 +434,12 @@
     takes(1, 1, (0, 1))
     takes(1, 0, (3,))
     takes(1, 2, (3,))
+
+    @pl.when(moves)
+    def _():
+        received(one_r.at[1], triangle)
+        mirror(new_stat)
+
     takes(1, 1, (2, 3))
     value = stage_take(1, 2)
     prec_sq = total(jnp.where(top & (lane == 0), value, 0.0))
@@ -499,7 +500,7 @@
 
 
 def place_kernel(blocks, gath, stat_in, scale, out, stat_out, stage, sem):
-    stat_copy = pltpu.make_async_copy(stat_in, stat_out, sem.at[8])
+    stat_copy = pltpu.make_async_copy(stat_in, stat_out, sem.at[16])
     stat_copy.start()
     copies = []
     for block in range(8):
@@ -508,10 +509,11 @@
             pair = jnp.where(blocks[0, p] == block, p, pair)
         slot = (pair // 4 + 2 * (pair % 2)) * 2 + (pair // 2) % 2
         for half in range(2):
-            stage[block, half * HALF : (half + 1) * HALF] = gath[slot * 2 + half] * scale[0:1, 0:1]
-        copy = pltpu.make_async_copy(stage.at[block], out.at[pl.ds(block * BLOCK, BLOCK)], sem.at[block])
-        copy.start()
-        copies.append(copy)
+            i = block * 2 + half
+            stage[i] = gath[slot * 2 + half] * scale[0:1, 0:1]
+            copy = pltpu.make_async_copy(stage.at[i], out.at[pl.ds(i * HALF, HALF)], sem.at[i])
+            copy.start()
+            copies.append(copy)
     for copy in copies:
         copy.wait()
     stat_copy.wait()
@@ -528,7 +530,7 @@
             jax.ShapeDtypeStruct((8 * BLOCK, BLOCK), f32),
             jax.ShapeDtypeStruct((BLOCK, BLOCK), f32),
         ),
-        scratch_shapes=[pltpu.VMEM((8, BLOCK, BLOCK), f32), pltpu.SemaphoreType.DMA((9,))],
+        scratch_shapes=[pltpu.VMEM((16, HALF, BLOCK), f32), pltpu.SemaphoreType.DMA((17,))],
         compiler_params=pltpu.CompilerParams(vmem_limit_bytes=24 * 1024 * 1024),
         name="place",
     )(blocks, gath, stat, scale)

time: 115 us -> 115 us (level)
  no operation moved by 1% of the time
where the time goes in v10:
time: 115 us; the launch traced here: 113 us
  Pallas kernels  112 us (97%)
    pallas_call x1, Pallas kernels, run_main(): pl.pallas_call(main_kernel, out_shape=(jax.ShapeDtypeStruct((16, HALF, BL...  108 us
    pallas_call x1, Pallas kernels, run_place(): pl.pallas_call(place_kernel, in_specs=[pl.BlockSpec(memory_space=pltpu.SM...  4.43 us

profile of v10, /device:TPU:1, one launch (start us, length us, event | category | flops | bytes accessed | tf_op | source)
XLA Modules:
  0.0 112.6 jit_solution(5325742929907234229)
XLA Ops:
  0.6 107.6 %shampoo.1 = (f32[16,256,512]{2,1,0:T(8,128)S(1)}, f32[512,512]{1,0:T(8,128)S(1)}, f32[8,128]{1,0:T(8,128)S(1)}) custom-call(s32[1,8]{1,0:T(1,128)} %blocks.3, bf16[256,4096]{1,0:T(8,128)(2,1)} %act_in.1, bf16[256,512]{1,0:T(8,128)(2,1)} %og_in.1, f32[512,512]{1,0:T(8,128)} %bitcast.2), custom_call_target="tpu_custom_call" | custom-call | tf_op jit(solution)/shard_map/shampoo/pallas_call | solution.py:466
  108.2 4.4 %place.1 = (f32[4096,512]{1,0:T(8,128)}, f32[512,512]{1,0:T(8,128)}) custom-call(s32[1,8]{1,0:T(1,128)} %blocks.3, f32[16,256,512]{2,1,0:T(8,128)S(1)} %get-tuple-element.7.gath, f32[512,512]{1,0:T(8,128)S(1)} %get-tuple-element.8.stat_in, f32[8,128]{1,0:T(8,128)S(1)} %get-tuple-element.9.scale), custom_call_target="tpu_custom_call" | custom-call | tf_op jit(solution)/shard_map/place/pallas_call | solution.py:525
